TPU v7x, 16 devices: a whole 2x2x2 slice. The times are simulated.
16 devices in a mesh: heads: 4 (over z, y), model: 4 (over x, core).
Axes of the slice: x: 2, y: 2, z: 2, core: 2. Of those that a mesh axis runs over, the one named last changes fastest.
Arguments:
- hidden_in: bfloat16 [4096, 2560], P(None, 'model')
- seg_ids: int32 [4096], replicated
- positions: int32 [4096], replicated
- w_query: bfloat16 [2, 2560, 2048], P(None, 'model', 'heads')
- w_key: bfloat16 [2, 2560, 1024], P(None, 'model', 'heads')
- w_value: bfloat16 [2, 2560, 1024], P(None, 'model', 'heads')
- w_out: bfloat16 [2, 2048, 2560], P(None, 'heads', 'model')
- w_gate: bfloat16 [2, 2560, 10240], P(None, 'model', 'heads')
- w_up: bfloat16 [2, 2560, 10240], P(None, 'model', 'heads')
- w_down: bfloat16 [2, 10240, 2560], P(None, 'heads', 'model')
- norm_scales: float32 [2, 4, 2560], P(None, None, 'model')
- qk_scales: float32 [2, 2, 256], replicated
Outputs:
- output 1: bfloat16 [4096, 2560], P(None, 'model')
- output 2: bfloat16 [2, 4096, 4, 256], P(None, None, 'heads')
- output 3: bfloat16 [2, 4096, 4, 256], P(None, None, 'heads')
All inputs are finite; a program needn't handle non-finite values.
Results may differ from a plain program's by a relative error of at most 0.02.
Values are sent between devices in bfloat16 or wider.
A program may use at most 1 GiB of HBM per device.

v0:
```python
import jax
import jax.numpy as jnp
from jax import lax
from jax.experimental import pallas as pl
from jax.experimental.pallas import tpu as pltpu
from jax.sharding import PartitionSpec as P

NORM_EPS = 1e-6
WINDOW = 1024
GLOBAL_BASE = 1000000.0
GLOBAL_FACTOR = 8.0
LOCAL_BASE = 10000.0
HEAD_DIM = 256
KEY_BLOCK = 512
Q_ROWS = 256
MASKED = -1e30


def rope_tables(positions, head_dim, rope_base, pos_factor):
    exponents = jnp.arange(0, head_dim, 2).astype(jnp.float32) / head_dim
    inv_freq = rope_base ** (-exponents)
    angles = (positions.astype(jnp.float32) / pos_factor)[:, None] * inv_freq[None, :]
    return jnp.cos(angles), jnp.sin(angles)


def norm_rows(values, scale_row):
    mean_sq = jnp.mean(values * values, axis=-1, keepdims=True)
    return values * lax.rsqrt(mean_sq + NORM_EPS) * (1.0 + scale_row)


def norm_rope(values_bf, scale_row, cos_tab, sin_tab):
    normed = norm_rows(values_bf.astype(jnp.float32), scale_row)
    half = normed.shape[-1] // 2
    first, second = normed[:, :half], normed[:, half:]
    return jnp.concatenate([first * cos_tab - second * sin_tab, second * cos_tab + first * sin_tab], axis=-1).astype(jnp.bfloat16)


def dot4(h_ref, w_refs):
    depth = w_refs[0].shape[0]
    total = None
    for j, w_ref in enumerate(w_refs):
        part = jnp.dot(h_ref[:, j * depth:(j + 1) * depth], w_ref[...], preferred_element_type=jnp.float32)
        total = part if total is None else total + part
    return total


def kv_kernel(h_ref, w0, w1, w2, w3, cos_ref, sin_ref, scale_ref, out_ref):
    acc = dot4(h_ref, (w0, w1, w2, w3)).astype(jnp.bfloat16)
    out_ref[:, :HEAD_DIM] = norm_rope(acc[:, :HEAD_DIM], scale_ref[...], cos_ref[...], sin_ref[...])
    out_ref[:, HEAD_DIM:] = acc[:, HEAD_DIM:]


def q_kernel(h_ref, w0, w1, w2, w3, cos_ref, sin_ref, scale_ref, out_ref):
    acc = dot4(h_ref, (w0, w1, w2, w3)).astype(jnp.bfloat16)
    for n in range(2):
        cols = slice(n * HEAD_DIM, (n + 1) * HEAD_DIM)
        out_ref[:, cols] = norm_rope(acc[:, cols], scale_ref[...], cos_ref[...], sin_ref[...])


def project(kernel, h_full, pieces, col_block, cos_tab, sin_tab, scale_row):
    n_tok, width = h_full.shape
    depth = pieces[0].shape[0]
    return pl.pallas_call(
        kernel,
        grid=(n_tok // Q_ROWS,),
        in_specs=[pl.BlockSpec((Q_ROWS, width), lambda i: (i, 0))]
        + [pl.BlockSpec((depth, 512), lambda i: (0, col_block))] * 4
        + [pl.BlockSpec((Q_ROWS, HEAD_DIM // 2), lambda i: (i, 0))] * 2
        + [pl.BlockSpec((1, HEAD_DIM), lambda i: (0, 0))],
        out_specs=pl.BlockSpec((Q_ROWS, 512), lambda i: (i, 0)),
        out_shape=jax.ShapeDtypeStruct((n_tok, 512), jnp.bfloat16),
        compiler_params=pltpu.CompilerParams(dimension_semantics=("arbitrary",)),
        cost_estimate=pl.CostEstimate(flops=2 * n_tok * width * 512, bytes_accessed=10_000_000, transcendentals=0),
    )(h_full, *pieces, cos_tab, sin_tab, scale_row)


def attention_kernel(bounds_ref, q_ref, k_ref, v_ref, low_ref, o_ref):
    step = pl.program_id(0)
    row_base = bounds_ref[0] + step * Q_ROWS
    first_block = bounds_ref[1 + step] // KEY_BLOCK
    last_block = (row_base + Q_ROWS + KEY_BLOCK - 1) // KEY_BLOCK
    q2 = jnp.concatenate([q_ref[:, :HEAD_DIM], q_ref[:, HEAD_DIM:]], axis=0)
    low = jnp.concatenate([low_ref[...], low_ref[...]], axis=0)
    rows = row_base + lax.broadcasted_iota(jnp.int32, (Q_ROWS, 1), 0)
    rows = jnp.concatenate([rows, rows], axis=0)
    scale = HEAD_DIM ** -0.5

    def one_block(block, carry):
        row_max, row_sum, acc = carry
        base = pl.multiple_of(block * KEY_BLOCK, KEY_BLOCK)
        k_blk = k_ref[pl.ds(base, KEY_BLOCK), :]
        v_blk = v_ref[pl.ds(base, KEY_BLOCK), :]
        scores = lax.dot_general(q2, k_blk, (((1,), (1,)), ((), ())), preferred_element_type=jnp.float32) * scale
        cols = base + lax.broadcasted_iota(jnp.int32, (1, KEY_BLOCK), 1)
        scores = jnp.where((cols >= low) & (cols <= rows), scores, MASKED)
        new_max = jnp.maximum(row_max, jnp.max(scores, axis=-1, keepdims=True))
        old = jnp.exp(row_max - new_max)
        probs = jnp.exp(scores - new_max)
        row_sum = row_sum * old + jnp.sum(probs, axis=-1, keepdims=True)
        acc = acc * old + jnp.dot(probs.astype(jnp.bfloat16), v_blk, preferred_element_type=jnp.float32)
        return new_max, row_sum, acc

    init = (jnp.full((2 * Q_ROWS, 1), 2 * MASKED, jnp.float32), jnp.zeros((2 * Q_ROWS, 1), jnp.float32),
            jnp.zeros((2 * Q_ROWS, HEAD_DIM), jnp.float32))
    _, row_sum, acc = lax.fori_loop(first_block, last_block, one_block, init)
    out = (acc / row_sum).astype(jnp.bfloat16)
    o_ref[:, :HEAD_DIM] = out[:Q_ROWS]
    o_ref[:, HEAD_DIM:] = out[Q_ROWS:]


def attend(q_loc, kv_all, low, bounds):
    n_q = q_loc.shape[0]
    n_tok = kv_all.shape[0]
    return pl.pallas_call(
        attention_kernel,
        grid_spec=pltpu.PrefetchScalarGridSpec(
            num_scalar_prefetch=1,
            grid=(n_q // Q_ROWS,),
            in_specs=[pl.BlockSpec((Q_ROWS, 512), lambda i, b: (i, 0)),
                      pl.BlockSpec((n_tok, HEAD_DIM), lambda i, b: (0, 0)),
                      pl.BlockSpec((n_tok, HEAD_DIM), lambda i, b: (0, 1)),
                      pl.BlockSpec((Q_ROWS, 1), lambda i, b: (i, 0))],
            out_specs=pl.BlockSpec((Q_ROWS, 512), lambda i, b: (i, 0))),
        out_shape=jax.ShapeDtypeStruct((n_q, 512), jnp.bfloat16),
        compiler_params=pltpu.CompilerParams(dimension_semantics=("arbitrary",)),
        cost_estimate=pl.CostEstimate(flops=2 * n_q * n_tok * 512, bytes_accessed=8_000_000, transcendentals=0),
    )(bounds, q_loc, kv_all, kv_all, low)


def ffn_up_kernel(h_ref, g0, g1, g2, g3, u0, u1, u2, u3, out_ref):
    def chunk(i, _):
        rows = pl.ds(pl.multiple_of(i * 256, 256), 256)
        h_rows = h_ref.at[rows, :]
        gate = dot4(h_rows, (g0, g1, g2, g3)).astype(jnp.bfloat16).astype(jnp.float32)
        up = dot4(h_rows, (u0, u1, u2, u3)).astype(jnp.bfloat16).astype(jnp.float32)
        out_ref[rows, :] = (jax.nn.gelu(gate, approximate=True) * up).astype(jnp.bfloat16)
        return 0

    lax.fori_loop(0, h_ref.shape[0] // 256, chunk, 0)


def ffn_up(h_full, gates, ups):
    n_tok, width = h_full.shape
    depth, n_cols = gates[0].shape
    block = 512
    return pl.pallas_call(
        ffn_up_kernel,
        grid=(n_cols // block,),
        in_specs=[pl.BlockSpec((n_tok, width), lambda n: (0, 0))] + [pl.BlockSpec((depth, block), lambda n: (0, n))] * 8,
        out_specs=pl.BlockSpec((n_tok, block), lambda n: (0, n)),
        out_shape=jax.ShapeDtypeStruct((n_tok, n_cols), jnp.bfloat16),
        compiler_params=pltpu.CompilerParams(dimension_semantics=("arbitrary",)),
        cost_estimate=pl.CostEstimate(flops=4 * n_tok * width * n_cols, bytes_accessed=40_000_000, transcendentals=n_tok * n_cols),
    )(h_full, *gates, *ups)


def pre_kernel(x0, x1, x2, x3, scale_ref, hidden_ref, h_ref):
    hidden = jnp.concatenate([x0[...], x1[...], x2[...], x3[...]], axis=1)
    hidden_ref[...] = hidden
    h_ref[...] = norm_rows(hidden.astype(jnp.float32), scale_ref[...]).astype(jnp.bfloat16)


def out_kernel(o0, o1, o2, o3, a0, a1, a2, a3, b0, b1, b2, b3, resid_ref, post_ref, next_ref, mid_ref, h2_ref):
    half = a0.shape[1] // 2
    near, far = None, None
    for o, a, b in zip((o0, o1, o2, o3), (a0, a1, a2, a3), (b0, b1, b2, b3)):
        part_a = jnp.dot(o[...], a[...], preferred_element_type=jnp.float32)
        part_b = jnp.dot(o[...], b[...], preferred_element_type=jnp.float32)
        near = part_a if near is None else near + part_a
        far = part_b if far is None else far + part_b
    attn = jnp.concatenate([near[:, :half], far[:, :half], near[:, half:], far[:, half:]], axis=1)
    attn = attn.astype(jnp.bfloat16).astype(jnp.float32)
    mid = (resid_ref[...].astype(jnp.float32) + norm_rows(attn, post_ref[...])).astype(jnp.bfloat16)
    mid_ref[...] = mid
    h2_ref[...] = norm_rows(mid.astype(jnp.float32), next_ref[...]).astype(jnp.bfloat16)


def post_kernel(f0, f1, f2, f3, mid_ref, post_ref, next_ref, hidden_ref, h_ref):
    ffn = jnp.concatenate([f0[...], f1[...], f2[...], f3[...]], axis=1).astype(jnp.bfloat16).astype(jnp.float32)
    hidden = (mid_ref[...].astype(jnp.float32) + norm_rows(ffn, post_ref[...])).astype(jnp.bfloat16)
    hidden_ref[...] = hidden
    h_ref[...] = norm_rows(hidden.astype(jnp.float32), next_ref[...]).astype(jnp.bfloat16)


def whole(kernel, n_out, rows, width, flops, *args):
    blk = 128
    full = lambda v: pl.BlockSpec(v.shape, lambda i: (0, 0))
    tiled = lambda v: pl.BlockSpec((blk, v.shape[1]), lambda i: (i, 0))
    return pl.pallas_call(
        kernel,
        grid=(rows // blk,),
        in_specs=[tiled(v) if v.shape[0] == rows else full(v) for v in args],
        out_specs=[pl.BlockSpec((blk, width), lambda i: (i, 0))] * n_out,
        out_shape=[jax.ShapeDtypeStruct((rows, width), jnp.bfloat16)] * n_out,
        compiler_params=pltpu.CompilerParams(dimension_semantics=("arbitrary",)),
        cost_estimate=pl.CostEstimate(flops=flops, bytes_accessed=8_000_000, transcendentals=0),
    )(*args)


def solution(mesh):
    col_spec = P(None, 'model', 'heads')
    row_spec = P(None, 'heads', 'model')
    cache_spec = P(None, None, 'heads', None)

    def swap(value, bits, axis='model'):
        return lax.ppermute(value, axis, [(i, i ^ bits) for i in range(4)])

    def gather_pieces(own):
        far = swap(own, 2)
        near = swap(own, 1)
        diag = swap(far, 1)
        return (own, near, far, diag)

    def gather_out(own):
        both = jnp.concatenate([own, swap(own, 2)], axis=-1)
        y = swap(both, 1, 'heads')
        z = swap(both, 2, 'heads')
        d = swap(y, 2, 'heads')
        a = (both, y, z, d)
        b = tuple(swap(v, 1) for v in a)
        return a, b

    def layers(hidden_in, seg_ids, positions, w_query, w_key, w_value, w_out, w_gate, w_up, w_down, norm_scales, qk_scales):
        n_tok, part = hidden_in.shape
        width = part * 4
        me = lax.axis_index('model')
        head = lax.axis_index('heads')
        rows_m = n_tok // 4
        rows_own = n_tok // 16

        scales_all = lax.all_gather(norm_scales, 'model')
        scales = jnp.concatenate([lax.dynamic_index_in_dim(scales_all, me ^ j, 0, keepdims=False) for j in range(4)], axis=-1)
        row = lambda l, i: scales[l, i:i + 1]

        xs = [lax.dynamic_slice(hidden_in, ((me ^ j) * rows_m + head * rows_own, 0), (rows_own, part)) for j in range(4)]
        xs = [xs[0]] + [swap(xs[j], j) for j in range(1, 4)]

        index = jnp.arange(n_tok, dtype=jnp.int32)
        starts = index - positions
        pos_loc = lax.dynamic_slice(positions, (me * rows_m,), (rows_m,))

        w_qkv = jnp.concatenate([w_query, w_key, w_value], axis=-1)
        pieces = []
        for l in range(2):
            pieces.append((gather_pieces(w_qkv[l]), gather_out(w_out[l]),
                           gather_pieces(w_gate[l]), gather_pieces(w_up[l]), gather_pieces(w_down[l])))

        hidden, normed = whole(pre_kernel, 2, rows_own, width, 100_000_000, *xs, row(0, 0))

        settings = ((GLOBAL_BASE, GLOBAL_FACTOR, n_tok), (LOCAL_BASE, 1.0, WINDOW))
        kv_list = []
        for l in range(2):
            rope_base, pos_factor, window = settings[l]
            qkv_p, (out_a, out_b), gate_p, up_p, down_p = pieces[l]
            cos_tab, sin_tab = rope_tables(pos_loc, HEAD_DIM, rope_base, pos_factor)
            h_full = lax.all_gather(normed, 'heads', axis=0, tiled=True)
            kv_loc = project(kv_kernel, h_full, qkv_p, 1, cos_tab, sin_tab, qk_scales[l, 1:2])
            kv_all = lax.all_gather(kv_loc, 'model', axis=0, tiled=True)
            q_loc = project(q_kernel, h_full, qkv_p, 0, cos_tab, sin_tab, qk_scales[l, 0:1])
            kv_list.append(kv_all)
            low_all = jnp.maximum(starts, index - (window - 1))
            low = lax.dynamic_slice(low_all, (me * rows_m,), (rows_m,))
            bounds = jnp.concatenate([(me * rows_m).astype(jnp.int32)[None], low[::Q_ROWS]])
            o_loc = attend(q_loc, kv_all, low[:, None], bounds)
            os = [lax.dynamic_slice(o_loc, ((head ^ j) * rows_own, 0), (rows_own, 512)) for j in range(4)]
            os = [os[0]] + [swap(os[j], j, 'heads') for j in range(1, 4)]
            mid, normed2 = whole(out_kernel, 2, rows_own, width, 2 * rows_own * 2048 * width, *os, *out_a, *out_b, hidden, row(l, 1), row(l, 2))
            h2_full = lax.all_gather(normed2, 'heads', axis=0, tiled=True)
            ffn_in = ffn_up(h2_full, gate_p, up_p)
            f_parts = [lax.psum_scatter(jnp.dot(ffn_in, w, preferred_element_type=jnp.float32), 'heads', scatter_dimension=0, tiled=True) for w in down_p]
            hidden, normed = whole(post_kernel, 2, rows_own, width, 100_000_000, *f_parts, mid, row(l, 3), row(1, 0))

        mine = [hidden[:, :part]] + [swap(hidden[:, j * part:(j + 1) * part], j) for j in range(1, 4)]
        stacked = jnp.stack(mine)
        ordered = jnp.stack([lax.dynamic_index_in_dim(stacked, me ^ j, 0, keepdims=False) for j in range(4)])
        full = lax.all_gather(ordered, 'heads', axis=1, tiled=True)
        hidden_out = full.reshape(n_tok, part)
        keys = jnp.stack([kv[:, :HEAD_DIM] for kv in kv_list])[:, :, None, :]
        values = jnp.stack([kv[:, HEAD_DIM:] for kv in kv_list])[:, :, None, :]
        return hidden_out, keys, values

    return jax.shard_map(layers, mesh=mesh,
                         in_specs=(P(None, 'model'), P(), P(), col_spec, col_spec, col_spec, row_spec, col_spec, col_spec, row_spec, P(None, None, 'model'), P()),
                         out_specs=(P(None, 'model'), cache_spec, cache_spec),
                         check_vma=False)
```

profile of v0, /device:TPU:0, one launch (start us, length us, event | category | flops | bytes accessed | tf_op | source)
XLA Modules:
  0.0 1284.9 jit_solution(16931350315466441217)
XLA Ops:
  12.9 16.6 %all-gather = f32[8,4,640]{2,1,0:T(4,128)S(1)} all-gather(f32[2,4,640]{2,1,0:T(4,128)} %param.21), channel_id=2, replica_groups=mesh['heads'=4,'model'=4] {'model'}, dimensions={0}, use_global_device_ids=true | all-gather | bytes 102400 | tf_op jit(solution)/shard_map/all_gather | solution.py:231
  36.5 29.3 %collective-permute-done.4.w2 = bf16[640,1024]{1,0:T(8,128)(2,1)} collective-permute-done((bf16[640,1024]{1,0:T(8,128)(2,1)S(1)}, bf16[640,1024]{1,0:T(8,128)(2,1)}, u32[]{:S(2)}, u32[]{:S(2)}) %collective-permute-start.4) | collective-permute-done | bytes 1310752 | tf_op jit(solution)/shard_map/ppermute | solution.py:206
  69.6 23.4 %all-gather.9.cloned.1.call-done.h_ref = bf16[1024,2560]{1,0:T(8,128)(2,1)} async-done(((bf16[256,2560]{1,0:T(8,128)(2,1)}), bf16[1024,2560]{1,0:T(8,128)(2,1)}) %all-gather.9.cloned.1.call-update) | async-done | bytes 5242896 | tf_op jit(solution)/shard_map/all_gather | solution.py:256
  93.0 7.8 shard_map.132
  103.8 25.4 %collective-permute-done.9 = bf16[512,640]{1,0:T(8,128)(2,1)S(1)} collective-permute-done((bf16[512,640]{1,0:T(8,128)(2,1)S(1)}, bf16[512,640]{1,0:T(8,128)(2,1)S(1)}, u32[]{:S(2)}, u32[]{:S(2)}) %collective-permute-start.9) | collective-permute-done | bytes 655392 | tf_op jit(solution)/shard_map/ppermute | solution.py:206
  130.7 25.6 %collective-permute-done.10.a1 = bf16[512,1280]{1,0:T(8,128)(2,1)} collective-permute-done((bf16[512,1280]{1,0:T(8,128)(2,1)S(1)}, bf16[512,1280]{1,0:T(8,128)(2,1)}, u32[]{:S(2)}, u32[]{:S(2)}) %collective-permute-start.10) | collective-permute-done | bytes 1310752 | tf_op jit(solution)/shard_map/ppermute | solution.py:206
  160.3 25.2 %collective-permute-done.12.a3 = bf16[512,1280]{1,0:T(8,128)(2,1)} collective-permute-done((bf16[512,1280]{1,0:T(8,128)(2,1)}, bf16[512,1280]{1,0:T(8,128)(2,1)}, u32[]{:S(2)}, u32[]{:S(2)}) %collective-permute-start.12) | collective-permute-done | bytes 1310752 | tf_op jit(solution)/shard_map/ppermute | solution.py:206
  187.3 7.9 shard_map.131.q_ref
  195.2 11.2 shard_map.133
  222.1 9.7 shard_map.134
  237.4 6.4 collective-permute-start.18
  251.1 64.6 %collective-permute-done.18.g2 = bf16[640,2560]{1,0:T(8,128)(2,1)S(1)} collective-permute-done((bf16[640,2560]{1,0:T(8,128)(2,1)S(1)}, bf16[640,2560]{1,0:T(8,128)(2,1)S(1)}, u32[]{:S(2)}, u32[]{:S(2)}) %collective-permute-start.18) | collective-permute-done | bytes 3276832 | tf_op jit(solution)/shard_map/ppermute | solution.py:206
  315.7 67.1 %collective-permute-done.21.u2 = bf16[640,2560]{1,0:T(8,128)(2,1)S(1)} collective-permute-done((bf16[640,2560]{1,0:T(8,128)(2,1)S(1)}, bf16[640,2560]{1,0:T(8,128)(2,1)S(1)}, u32[]{:S(2)}, u32[]{:S(2)}) %collective-permute-start.21) | collective-permute-done | bytes 3276832 | tf_op jit(solution)/shard_map/ppermute | solution.py:206
  388.8 41.9 %shard_map.135 = bf16[1024,2560]{1,0:T(8,128)(2,1)} custom-call(bf16[1024,2560]{1,0:T(8,128)(2,1)} %all-gather.13.cloned.1.call-done.h_ref, bf16[640,2560]{1,0:T(8,128)(2,1)} %copy-done.9, bf16[640,2560]{1,0:T(8,128)(2,1)} %copy-done.30, bf16[640,2560]{1,0:T(8,128)(2,1)} %copy-done.26, bf16[640,2560]{1,0:T(8,128)(2,1)} %copy-done.34, ...), custom_call_target="tpu_custom_call" | custom-call | flops 26843545600 | bytes 40000000 | tf_op jit(solution)/shard_map/pallas_call | solution.py:146
  430.7 9.2 fusion.5
  447.1 5.7 collective-permute-done.23
  452.8 8.4 fusion.7
  462.1 72.4 %collective-permute-done.24 = bf16[2560,640]{1,0:T(8,128)(2,1)S(1)} collective-permute-done((bf16[2560,640]{1,0:T(8,128)(2,1)}, bf16[2560,640]{1,0:T(8,128)(2,1)S(1)}, u32[]{:S(2)}, u32[]{:S(2)}) %collective-permute-start.24) | collective-permute-done | bytes 3276832 | tf_op jit(solution)/shard_map/ppermute | solution.py:206
  536.2 8.2 fusion.8
  544.7 6.0 collective-permute-done.25
  550.8 8.3 fusion.9
  559.2 21.0 %reduce-scatter.13.cloned.1.call-done.f2 = f32[256,640]{1,0:T(8,128)} async-done(((f32[1024,640]{1,0:T(8,128)}), f32[256,640]{1,0:T(8,128)}) %reduce-scatter.13.cloned.1.call-update) | async-done | bytes 655376 | tf_op jit(solution)/shard_map/reduce_scatter | solution.py:270
  580.2 38.8 %reduce-scatter.15.cloned.1.call-done.f3 = f32[256,640]{1,0:T(8,128)} async-done(((f32[1024,640]{1,0:T(8,128)}), f32[256,640]{1,0:T(8,128)}) %reduce-scatter.15.cloned.1.call-update) | async-done | bytes 655376 | tf_op jit(solution)/shard_map/reduce_scatter | solution.py:270
  624.2 28.9 %collective-permute-done.27.w2 = bf16[640,1024]{1,0:T(8,128)(2,1)S(1)} collective-permute-done((bf16[640,1024]{1,0:T(8,128)(2,1)S(1)}, bf16[640,1024]{1,0:T(8,128)(2,1)S(1)}, u32[]{:S(2)}, u32[]{:S(2)}) %collective-permute-start.27) | collective-permute-done | bytes 1310752 | tf_op jit(solution)/shard_map/ppermute | solution.py:206
  657.3 23.1 %all-gather.15.cloned.1.call-done.h_ref = bf16[1024,2560]{1,0:T(8,128)(2,1)} async-done(((bf16[256,2560]{1,0:T(8,128)(2,1)}), bf16[1024,2560]{1,0:T(8,128)(2,1)}) %all-gather.15.cloned.1.call-update) | async-done | bytes 5242896 | tf_op jit(solution)/shard_map/all_gather | solution.py:256
  680.4 7.8 shard_map.138
  689.8 24.0 %collective-permute-done.32 = bf16[512,640]{1,0:T(8,128)(2,1)S(1)} collective-permute-done((bf16[512,640]{1,0:T(8,128)(2,1)S(1)}, bf16[512,640]{1,0:T(8,128)(2,1)S(1)}, u32[]{:S(2)}, u32[]{:S(2)}) %collective-permute-start.32) | collective-permute-done | bytes 655392 | tf_op jit(solution)/shard_map/ppermute | solution.py:206
  715.3 25.5 %collective-permute-done.33.a1 = bf16[512,1280]{1,0:T(8,128)(2,1)S(1)} collective-permute-done((bf16[512,1280]{1,0:T(8,128)(2,1)S(1)}, bf16[512,1280]{1,0:T(8,128)(2,1)S(1)}, u32[]{:S(2)}, u32[]{:S(2)}) %collective-permute-start.33) | collective-permute-done | bytes 1310752 | tf_op jit(solution)/shard_map/ppermute | solution.py:206
  745.1 25.0 %collective-permute-done.35.a3 = bf16[512,1280]{1,0:T(8,128)(2,1)} collective-permute-done((bf16[512,1280]{1,0:T(8,128)(2,1)S(1)}, bf16[512,1280]{1,0:T(8,128)(2,1)}, u32[]{:S(2)}, u32[]{:S(2)}) %collective-permute-start.35) | collective-permute-done | bytes 1310752 | tf_op jit(solution)/shard_map/ppermute | solution.py:206
  771.8 7.9 shard_map.137.q_ref
  779.8 11.2 shard_map.139
  806.7 9.8 shard_map.140
  816.8 6.5 collective-permute-start.41
  823.8 71.2 %collective-permute-done.41.g2 = bf16[640,2560]{1,0:T(8,128)(2,1)S(1)} collective-permute-done((bf16[640,2560]{1,0:T(8,128)(2,1)S(1)}, bf16[640,2560]{1,0:T(8,128)(2,1)S(1)}, u32[]{:S(2)}, u32[]{:S(2)}) %collective-permute-start.41) | collective-permute-done | bytes 3276832 | tf_op jit(solution)/shard_map/ppermute | solution.py:206
  895.0 67.1 %collective-permute-done.44.u2 = bf16[640,2560]{1,0:T(8,128)(2,1)S(1)} collective-permute-done((bf16[640,2560]{1,0:T(8,128)(2,1)}, bf16[640,2560]{1,0:T(8,128)(2,1)S(1)}, u32[]{:S(2)}, u32[]{:S(2)}) %collective-permute-start.44) | collective-permute-done | bytes 3276832 | tf_op jit(solution)/shard_map/ppermute | solution.py:206
  968.1 41.9 %shard_map.141 = bf16[1024,2560]{1,0:T(8,128)(2,1)} custom-call(bf16[1024,2560]{1,0:T(8,128)(2,1)} %all-gather.19.cloned.1.call-done.h_ref, bf16[640,2560]{1,0:T(8,128)(2,1)} %get-tuple-element.36.g0, bf16[640,2560]{1,0:T(8,128)(2,1)} %copy-done.31, bf16[640,2560]{1,0:T(8,128)(2,1)} %copy-done.27, bf16[640,2560]{1,0:T(8,128)(2,1)} %copy-done.35, ...), custom_call_target="tpu_custom_call" | custom-call | flops 26843545600 | bytes 40000000 | tf_op jit(solution)/shard_map/pallas_call | solution.py:146
  1010.0 9.3 fusion.6
  1019.6 5.7 collective-permute-done.46
  1025.3 8.2 fusion.10
  1034.5 72.1 %collective-permute-done.47 = bf16[2560,640]{1,0:T(8,128)(2,1)S(1)} collective-permute-done((bf16[2560,640]{1,0:T(8,128)(2,1)S(1)}, bf16[2560,640]{1,0:T(8,128)(2,1)S(1)}, u32[]{:S(2)}, u32[]{:S(2)}) %collective-permute-start.47) | collective-permute-done | bytes 3276832 | tf_op jit(solution)/shard_map/ppermute | solution.py:206
  1108.3 8.2 fusion.11
  1116.9 6.0 collective-permute-done.48
  1123.0 8.2 fusion.12
  1131.3 21.1 %reduce-scatter.21.cloned.1.call-done.f2 = f32[256,640]{1,0:T(8,128)} async-done(((f32[1024,640]{1,0:T(8,128)}), f32[256,640]{1,0:T(8,128)}) %reduce-scatter.21.cloned.1.call-update) | async-done | bytes 655376 | tf_op jit(solution)/shard_map/reduce_scatter | solution.py:270
  1152.4 39.2 %reduce-scatter.23.cloned.1.call-done.f3 = f32[256,640]{1,0:T(8,128)} async-done(((f32[1024,640]{1,0:T(8,128)}), f32[256,640]{1,0:T(8,128)}) %reduce-scatter.23.cloned.1.call-update) | async-done | bytes 655376 | tf_op jit(solution)/shard_map/reduce_scatter | solution.py:270
  1198.6 8.1 collective-permute-done.51
  1206.7 7.1 collective-permute-done.50
  1223.2 49.5 %all-gather.21.cloned.1.call-done = bf16[4,1024,640]{2,1,0:T(8,128)(2,1)} async-done(((bf16[4,256,640]{2,1,0:T(8,128)(2,1)}), bf16[4,1024,640]{2,1,0:T(8,128)(2,1)}) %all-gather.21.cloned.1.call-update) | async-done | bytes 5242896 | tf_op jit(solution)/shard_map/all_gather | solution.py:276
  (237 shorter events, 137.1 us)
Async XLA Ops:
  7.2 85.8 %all-gather.9.cloned.1.call-start = ((), (), s32[]{:S(2)}) async-start(), calls=%async_computation.8 | async-start | bytes 6553600 | tf_op jit(solution)/shard_map/all_gather | solution.py:256
  9.6 20.6 %collective-permute-start = (bf16[256,640]{1,0:T(8,128)(2,1)}, bf16[256,640]{1,0:T(8,128)(2,1)S(1)}, u32[]{:S(2)}, u32[]{:S(2)}) collective-permute-start(bf16[256,640]{1,0:T(8,128)(2,1)} %get-tuple-element.39), channel_id=1, source_target_pairs={{0,1},{1,0},{2,3},{3,2},{4,5},{5,4},{6,7},{7,6},{8,9},{9,8},{10,11... | collective-permute-start | bytes 983048 | tf_op jit(solution)/shard_map/ppermute | solution.py:206
  34.0 161.2 %all-gather.11.cloned.1.call-start = ((), (), s32[]{:S(2)}) async-start(), calls=%async_computation.9 | async-start | bytes 5242880 | tf_op jit(solution)/shard_map/all_gather | solution.py:258
  34.7 31.2 %collective-permute-start.4 = (bf16[640,1024]{1,0:T(8,128)(2,1)S(1)}, bf16[640,1024]{1,0:T(8,128)(2,1)}, u32[]{:S(2)}, u32[]{:S(2)}) collective-permute-start(bf16[640,1024]{1,0:T(8,128)(2,1)S(1)} %get-tuple-element.47.w0), channel_id=1, source_target_pairs={{0,2},{1,3},{2,0},{3,1},{4,6},{5,7},{6,4},{7,5},{8,10},{9,11},{10,... | collective-permute-start | bytes 3932168 | tf_op jit(solution)/shard_map/ppermute | solution.py:206
  36.5 33.1 %collective-permute-start.3 = (bf16[640,1024]{1,0:T(8,128)(2,1)S(1)}, bf16[640,1024]{1,0:T(8,128)(2,1)}, u32[]{:S(2)}, u32[]{:S(2)}) collective-permute-start(bf16[640,1024]{1,0:T(8,128)(2,1)S(1)} %get-tuple-element.47.w0), channel_id=1, source_target_pairs={{0,1},{1,0},{2,3},{3,2},{4,5},{5,4},{6,7},{7,6},{8,9},{9,8},{10,11... | collective-permute-start | bytes 3932168 | tf_op jit(solution)/shard_map/ppermute | solution.py:206
  100.8 287.9 %all-gather.13.cloned.1.call-start = ((), (), s32[]{:S(2)}) async-start(), calls=%async_computation.10 | async-start | bytes 6553600 | tf_op jit(solution)/shard_map/all_gather | solution.py:268
  102.3 26.9 %collective-permute-start.9 = (bf16[512,640]{1,0:T(8,128)(2,1)S(1)}, bf16[512,640]{1,0:T(8,128)(2,1)S(1)}, u32[]{:S(2)}, u32[]{:S(2)}) collective-permute-start(bf16[512,640]{1,0:T(8,128)(2,1)S(1)} %get-tuple-element.57), channel_id=1, source_target_pairs={{0,2},{1,3},{2,0},{3,1},{4,6},{5,7},{6,4},{7,5},{8,10},{9,11},{10,... | collective-permute-start | bytes 1966088 | tf_op jit(solution)/shard_map/ppermute | solution.py:206
  129.3 27.0 %collective-permute-start.10 = (bf16[512,1280]{1,0:T(8,128)(2,1)S(1)}, bf16[512,1280]{1,0:T(8,128)(2,1)}, u32[]{:S(2)}, u32[]{:S(2)}) collective-permute-start(bf16[512,1280]{1,0:T(8,128)(2,1)S(1)} %pad_maximum_fusion.a0), channel_id=1, source_target_pairs={{0,4},{4,0},{8,12},{12,8},{1,5},{5,1},{9,13},{13,9},{2,6},{6,2},{1... | collective-permute-start | bytes 3932168 | tf_op jit(solution)/shard_map/ppermute | solution.py:206
  130.6 29.7 %collective-permute-start.11 = (bf16[512,1280]{1,0:T(8,128)(2,1)S(1)}, bf16[512,1280]{1,0:T(8,128)(2,1)}, u32[]{:S(2)}, u32[]{:S(2)}) collective-permute-start(bf16[512,1280]{1,0:T(8,128)(2,1)S(1)} %pad_maximum_fusion.a0), channel_id=1, source_target_pairs={{0,8},{4,12},{8,0},{12,4},{1,9},{5,13},{9,1},{13,5},{2,10},{6,14},... | collective-permute-start | bytes 3932168 | tf_op jit(solution)/shard_map/ppermute | solution.py:206
  156.3 29.2 %collective-permute-start.12 = (bf16[512,1280]{1,0:T(8,128)(2,1)}, bf16[512,1280]{1,0:T(8,128)(2,1)}, u32[]{:S(2)}, u32[]{:S(2)}) collective-permute-start(bf16[512,1280]{1,0:T(8,128)(2,1)} %collective-permute-done.10.a1), channel_id=1, source_target_pairs={{0,8},{4,12},{8,0},{12,4},{1,9},{5,13},{9,1},{13,5},{2,10},{6,14},... | collective-permute-start | bytes 3932168 | tf_op jit(solution)/shard_map/ppermute | solution.py:206
  157.7 51.3 %collective-permute-start.13 = (bf16[512,1280]{1,0:T(8,128)(2,1)S(1)}, bf16[512,1280]{1,0:T(8,128)(2,1)}, u32[]{:S(2)}, u32[]{:S(2)}) collective-permute-start(bf16[512,1280]{1,0:T(8,128)(2,1)S(1)} %pad_maximum_fusion.a0), channel_id=1, source_target_pairs={{0,1},{1,0},{2,3},{3,2},{4,5},{5,4},{6,7},{7,6},{8,9},{9,8},{10,11... | collective-permute-start | bytes 3932168 | tf_op jit(solution)/shard_map/ppermute | solution.py:206
  157.7 52.7 %collective-permute-start.14 = (bf16[512,1280]{1,0:T(8,128)(2,1)}, bf16[512,1280]{1,0:T(8,128)(2,1)}, u32[]{:S(2)}, u32[]{:S(2)}) collective-permute-start(bf16[512,1280]{1,0:T(8,128)(2,1)} %collective-permute-done.10.a1), channel_id=1, source_target_pairs={{0,1},{1,0},{2,3},{3,2},{4,5},{5,4},{6,7},{7,6},{8,9},{9,8},{10,11... | collective-permute-start | bytes 3932168 | tf_op jit(solution)/shard_map/ppermute | solution.py:206
  160.3 51.6 %collective-permute-start.15 = (bf16[512,1280]{1,0:T(8,128)(2,1)}, bf16[512,1280]{1,0:T(8,128)(2,1)}, u32[]{:S(2)}, u32[]{:S(2)}) collective-permute-start(bf16[512,1280]{1,0:T(8,128)(2,1)} %collective-permute-done.11.a2), channel_id=1, source_target_pairs={{0,1},{1,0},{2,3},{3,2},{4,5},{5,4},{6,7},{7,6},{8,9},{9,8},{10,11... | collective-permute-start | bytes 3932168 | tf_op jit(solution)/shard_map/ppermute | solution.py:206
  185.5 26.4 %collective-permute-start.16 = (bf16[512,1280]{1,0:T(8,128)(2,1)}, bf16[512,1280]{1,0:T(8,128)(2,1)}, u32[]{:S(2)}, u32[]{:S(2)}) collective-permute-start(bf16[512,1280]{1,0:T(8,128)(2,1)} %collective-permute-done.12.a3), channel_id=1, source_target_pairs={{0,1},{1,0},{2,3},{3,2},{4,5},{5,4},{6,7},{7,6},{8,9},{9,8},{10,11... | collective-permute-start | bytes 3932168 | tf_op jit(solution)/shard_map/ppermute | solution.py:206
  231.8 327.4 %reduce-scatter.9.cloned.1.call-start = ((), (), s32[]{:S(2)}) async-start(), calls=%async_computation.11 | async-start | bytes 3276800 | tf_op jit(solution)/shard_map/reduce_scatter | solution.py:270
  237.4 78.2 %collective-permute-start.18 = (bf16[640,2560]{1,0:T(8,128)(2,1)S(1)}, bf16[640,2560]{1,0:T(8,128)(2,1)S(1)}, u32[]{:S(2)}, u32[]{:S(2)}) collective-permute-start(bf16[640,2560]{1,0:T(8,128)(2,1)S(1)} %get-tuple-element.37.g0), channel_id=1, source_target_pairs={{0,2},{1,3},{2,0},{3,1},{4,6},{5,7},{6,4},{7,5},{8,10},{9,11},{10,... | collective-permute-start | bytes 9830408 | tf_op jit(solution)/shard_map/ppermute | solution.py:206
  249.2 133.6 %collective-permute-start.21 = (bf16[640,2560]{1,0:T(8,128)(2,1)S(1)}, bf16[640,2560]{1,0:T(8,128)(2,1)S(1)}, u32[]{:S(2)}, u32[]{:S(2)}) collective-permute-start(bf16[640,2560]{1,0:T(8,128)(2,1)S(1)} %get-tuple-element.35.u0), channel_id=1, source_target_pairs={{0,2},{1,3},{2,0},{3,1},{4,6},{5,7},{6,4},{7,5},{8,10},{9,11},{10,... | collective-permute-start | bytes 9830408 | tf_op jit(solution)/shard_map/ppermute | solution.py:206
  250.6 132.3 %collective-permute-start.17 = (bf16[640,2560]{1,0:T(8,128)(2,1)S(1)}, bf16[640,2560]{1,0:T(8,128)(2,1)S(1)}, u32[]{:S(2)}, u32[]{:S(2)}) collective-permute-start(bf16[640,2560]{1,0:T(8,128)(2,1)S(1)} %get-tuple-element.37.g0), channel_id=1, source_target_pairs={{0,1},{1,0},{2,3},{3,2},{4,5},{5,4},{6,7},{7,6},{8,9},{9,8},{10,11... | collective-permute-start | bytes 9830408 | tf_op jit(solution)/shard_map/ppermute | solution.py:206
  250.6 132.3 %collective-permute-start.20 = (bf16[640,2560]{1,0:T(8,128)(2,1)S(1)}, bf16[640,2560]{1,0:T(8,128)(2,1)S(1)}, u32[]{:S(2)}, u32[]{:S(2)}) collective-permute-start(bf16[640,2560]{1,0:T(8,128)(2,1)S(1)} %get-tuple-element.35.u0), channel_id=1, source_target_pairs={{0,1},{1,0},{2,3},{3,2},{4,5},{5,4},{6,7},{7,6},{8,9},{9,8},{10,11... | collective-permute-start | bytes 9830408 | tf_op jit(solution)/shard_map/ppermute | solution.py:206
  315.7 67.2 %collective-permute-start.19 = (bf16[640,2560]{1,0:T(8,128)(2,1)S(1)}, bf16[640,2560]{1,0:T(8,128)(2,1)S(1)}, u32[]{:S(2)}, u32[]{:S(2)}) collective-permute-start(bf16[640,2560]{1,0:T(8,128)(2,1)S(1)} %collective-permute-done.18.g2), channel_id=1, source_target_pairs={{0,1},{1,0},{2,3},{3,2},{4,5},{5,4},{6,7},{7,6},{8,9},{9,8},{10,11... | collective-permute-start | bytes 9830408 | tf_op jit(solution)/shard_map/ppermute | solution.py:206
  439.9 119.3 %reduce-scatter.11.cloned.1.call-start = ((), (), s32[]{:S(2)}) async-start(), calls=%async_computation.12 | async-start | bytes 3276800 | tf_op jit(solution)/shard_map/reduce_scatter | solution.py:270
  461.2 119.0 %reduce-scatter.13.cloned.1.call-start = ((), (), s32[]{:S(2)}) async-start(), calls=%async_computation.13 | async-start | bytes 3276800 | tf_op jit(solution)/shard_map/reduce_scatter | solution.py:270
  461.2 73.2 %collective-permute-start.24 = (bf16[2560,640]{1,0:T(8,128)(2,1)}, bf16[2560,640]{1,0:T(8,128)(2,1)S(1)}, u32[]{:S(2)}, u32[]{:S(2)}) collective-permute-start(bf16[2560,640]{1,0:T(8,128)(2,1)} %copy-done.11), channel_id=1, source_target_pairs={{0,2},{1,3},{2,0},{3,1},{4,6},{5,7},{6,4},{7,5},{8,10},{9,11},{10,... | collective-permute-start | bytes 9830408 | tf_op jit(solution)/shard_map/ppermute | solution.py:206
  544.5 74.6 %reduce-scatter.15.cloned.1.call-start = ((), (), s32[]{:S(2)}) async-start(), calls=%async_computation.14 | async-start | bytes 3276800 | tf_op jit(solution)/shard_map/reduce_scatter | solution.py:270
  559.1 121.3 %all-gather.15.cloned.1.call-start = ((), (), s32[]{:S(2)}) async-start(), calls=%async_computation.15 | async-start | bytes 6553600 | tf_op jit(solution)/shard_map/all_gather | solution.py:256
  622.7 157.1 %all-gather.17.cloned.1.call-start = ((), (), s32[]{:S(2)}) async-start(), calls=%async_computation.16 | async-start | bytes 5242880 | tf_op jit(solution)/shard_map/all_gather | solution.py:258
  622.7 30.4 %collective-permute-start.27 = (bf16[640,1024]{1,0:T(8,128)(2,1)S(1)}, bf16[640,1024]{1,0:T(8,128)(2,1)S(1)}, u32[]{:S(2)}, u32[]{:S(2)}) collective-permute-start(bf16[640,1024]{1,0:T(8,128)(2,1)S(1)} %get-tuple-element.46.w0), channel_id=1, source_target_pairs={{0,2},{1,3},{2,0},{3,1},{4,6},{5,7},{6,4},{7,5},{8,10},{9,11},{10,... | collective-permute-start | bytes 3932168 | tf_op jit(solution)/shard_map/ppermute | solution.py:206
  624.2 32.0 %collective-permute-start.26 = (bf16[640,1024]{1,0:T(8,128)(2,1)S(1)}, bf16[640,1024]{1,0:T(8,128)(2,1)S(1)}, u32[]{:S(2)}, u32[]{:S(2)}) collective-permute-start(bf16[640,1024]{1,0:T(8,128)(2,1)S(1)} %get-tuple-element.46.w0), channel_id=1, source_target_pairs={{0,1},{1,0},{2,3},{3,2},{4,5},{5,4},{6,7},{7,6},{8,9},{9,8},{10,11... | collective-permute-start | bytes 3932168 | tf_op jit(solution)/shard_map/ppermute | solution.py:206
  688.2 279.9 %all-gather.19.cloned.1.call-start = ((), (), s32[]{:S(2)}) async-start(), calls=%async_computation.17 | async-start | bytes 6553600 | tf_op jit(solution)/shard_map/all_gather | solution.py:268
  688.3 25.5 %collective-permute-start.32 = (bf16[512,640]{1,0:T(8,128)(2,1)S(1)}, bf16[512,640]{1,0:T(8,128)(2,1)S(1)}, u32[]{:S(2)}, u32[]{:S(2)}) collective-permute-start(bf16[512,640]{1,0:T(8,128)(2,1)S(1)} %get-tuple-element.56), channel_id=1, source_target_pairs={{0,2},{1,3},{2,0},{3,1},{4,6},{5,7},{6,4},{7,5},{8,10},{9,11},{10,... | collective-permute-start | bytes 1966088 | tf_op jit(solution)/shard_map/ppermute | solution.py:206
  713.9 26.9 %collective-permute-start.33 = (bf16[512,1280]{1,0:T(8,128)(2,1)S(1)}, bf16[512,1280]{1,0:T(8,128)(2,1)S(1)}, u32[]{:S(2)}, u32[]{:S(2)}) collective-permute-start(bf16[512,1280]{1,0:T(8,128)(2,1)S(1)} %pad_maximum_fusion.1.a0), channel_id=1, source_target_pairs={{0,4},{4,0},{8,12},{12,8},{1,5},{5,1},{9,13},{13,9},{2,6},{6,2},{1... | collective-permute-start | bytes 3932168 | tf_op jit(solution)/shard_map/ppermute | solution.py:206
  715.2 29.9 %collective-permute-start.34 = (bf16[512,1280]{1,0:T(8,128)(2,1)S(1)}, bf16[512,1280]{1,0:T(8,128)(2,1)}, u32[]{:S(2)}, u32[]{:S(2)}) collective-permute-start(bf16[512,1280]{1,0:T(8,128)(2,1)S(1)} %pad_maximum_fusion.1.a0), channel_id=1, source_target_pairs={{0,8},{4,12},{8,0},{12,4},{1,9},{5,13},{9,1},{13,5},{2,10},{6,14},... | collective-permute-start | bytes 3932168 | tf_op jit(solution)/shard_map/ppermute | solution.py:206
  740.8 29.3 %collective-permute-start.35 = (bf16[512,1280]{1,0:T(8,128)(2,1)S(1)}, bf16[512,1280]{1,0:T(8,128)(2,1)}, u32[]{:S(2)}, u32[]{:S(2)}) collective-permute-start(bf16[512,1280]{1,0:T(8,128)(2,1)S(1)} %collective-permute-done.33.a1), channel_id=1, source_target_pairs={{0,8},{4,12},{8,0},{12,4},{1,9},{5,13},{9,1},{13,5},{2,10},{6,14},... | collective-permute-start | bytes 3932168 | tf_op jit(solution)/shard_map/ppermute | solution.py:206
  742.2 51.4 %collective-permute-start.36 = (bf16[512,1280]{1,0:T(8,128)(2,1)S(1)}, bf16[512,1280]{1,0:T(8,128)(2,1)}, u32[]{:S(2)}, u32[]{:S(2)}) collective-permute-start(bf16[512,1280]{1,0:T(8,128)(2,1)S(1)} %pad_maximum_fusion.1.a0), channel_id=1, source_target_pairs={{0,1},{1,0},{2,3},{3,2},{4,5},{5,4},{6,7},{7,6},{8,9},{9,8},{10,11... | collective-permute-start | bytes 3932168 | tf_op jit(solution)/shard_map/ppermute | solution.py:206
  742.2 52.8 %collective-permute-start.37 = (bf16[512,1280]{1,0:T(8,128)(2,1)S(1)}, bf16[512,1280]{1,0:T(8,128)(2,1)}, u32[]{:S(2)}, u32[]{:S(2)}) collective-permute-start(bf16[512,1280]{1,0:T(8,128)(2,1)S(1)} %collective-permute-done.33.a1), channel_id=1, source_target_pairs={{0,1},{1,0},{2,3},{3,2},{4,5},{5,4},{6,7},{7,6},{8,9},{9,8},{10,11... | collective-permute-start | bytes 3932168 | tf_op jit(solution)/shard_map/ppermute | solution.py:206
  745.1 51.3 %collective-permute-start.38 = (bf16[512,1280]{1,0:T(8,128)(2,1)}, bf16[512,1280]{1,0:T(8,128)(2,1)}, u32[]{:S(2)}, u32[]{:S(2)}) collective-permute-start(bf16[512,1280]{1,0:T(8,128)(2,1)} %collective-permute-done.34.a2), channel_id=1, source_target_pairs={{0,1},{1,0},{2,3},{3,2},{4,5},{5,4},{6,7},{7,6},{8,9},{9,8},{10,11... | collective-permute-start | bytes 3932168 | tf_op jit(solution)/shard_map/ppermute | solution.py:206
  770.1 26.4 %collective-permute-start.39 = (bf16[512,1280]{1,0:T(8,128)(2,1)}, bf16[512,1280]{1,0:T(8,128)(2,1)}, u32[]{:S(2)}, u32[]{:S(2)}) collective-permute-start(bf16[512,1280]{1,0:T(8,128)(2,1)} %collective-permute-done.35.a3), channel_id=1, source_target_pairs={{0,1},{1,0},{2,3},{3,2},{4,5},{5,4},{6,7},{7,6},{8,9},{9,8},{10,11... | collective-permute-start | bytes 3932168 | tf_op jit(solution)/shard_map/ppermute | solution.py:206
  816.5 314.8 %reduce-scatter.17.cloned.1.call-start = ((), (), s32[]{:S(2)}) async-start(), calls=%async_computation.18 | async-start | bytes 3276800 | tf_op jit(solution)/shard_map/reduce_scatter | solution.py:270
  816.8 78.3 %collective-permute-start.41 = (bf16[640,2560]{1,0:T(8,128)(2,1)S(1)}, bf16[640,2560]{1,0:T(8,128)(2,1)S(1)}, u32[]{:S(2)}, u32[]{:S(2)}) collective-permute-start(bf16[640,2560]{1,0:T(8,128)(2,1)S(1)} %copy-done.7), channel_id=1, source_target_pairs={{0,2},{1,3},{2,0},{3,1},{4,6},{5,7},{6,4},{7,5},{8,10},{9,11},{10,... | collective-permute-start | bytes 9830408 | tf_op jit(solution)/shard_map/ppermute | solution.py:206
  823.3 138.9 %collective-permute-start.44 = (bf16[640,2560]{1,0:T(8,128)(2,1)}, bf16[640,2560]{1,0:T(8,128)(2,1)S(1)}, u32[]{:S(2)}, u32[]{:S(2)}) collective-permute-start(bf16[640,2560]{1,0:T(8,128)(2,1)} %get-tuple-element.34.u0), channel_id=1, source_target_pairs={{0,2},{1,3},{2,0},{3,1},{4,6},{5,7},{6,4},{7,5},{8,10},{9,11},{10,... | collective-permute-start | bytes 9830408 | tf_op jit(solution)/shard_map/ppermute | solution.py:206
  823.3 138.9 %collective-permute-start.40 = (bf16[640,2560]{1,0:T(8,128)(2,1)S(1)}, bf16[640,2560]{1,0:T(8,128)(2,1)S(1)}, u32[]{:S(2)}, u32[]{:S(2)}) collective-permute-start(bf16[640,2560]{1,0:T(8,128)(2,1)S(1)} %copy-done.7), channel_id=1, source_target_pairs={{0,1},{1,0},{2,3},{3,2},{4,5},{5,4},{6,7},{7,6},{8,9},{9,8},{10,11... | collective-permute-start | bytes 9830408 | tf_op jit(solution)/shard_map/ppermute | solution.py:206
  823.3 138.9 %collective-permute-start.43 = (bf16[640,2560]{1,0:T(8,128)(2,1)}, bf16[640,2560]{1,0:T(8,128)(2,1)S(1)}, u32[]{:S(2)}, u32[]{:S(2)}) collective-permute-start(bf16[640,2560]{1,0:T(8,128)(2,1)} %get-tuple-element.34.u0), channel_id=1, source_target_pairs={{0,1},{1,0},{2,3},{3,2},{4,5},{5,4},{6,7},{7,6},{8,9},{9,8},{10,11... | collective-permute-start | bytes 9830408 | tf_op jit(solution)/shard_map/ppermute | solution.py:206
  895.0 67.2 %collective-permute-start.42 = (bf16[640,2560]{1,0:T(8,128)(2,1)S(1)}, bf16[640,2560]{1,0:T(8,128)(2,1)S(1)}, u32[]{:S(2)}, u32[]{:S(2)}) collective-permute-start(bf16[640,2560]{1,0:T(8,128)(2,1)S(1)} %collective-permute-done.41.g2), channel_id=1, source_target_pairs={{0,1},{1,0},{2,3},{3,2},{4,5},{5,4},{6,7},{7,6},{8,9},{9,8},{10,11... | collective-permute-start | bytes 9830408 | tf_op jit(solution)/shard_map/ppermute | solution.py:206
  1019.4 111.9 %reduce-scatter.19.cloned.1.call-start = ((), (), s32[]{:S(2)}) async-start(), calls=%async_computation.19 | async-start | bytes 3276800 | tf_op jit(solution)/shard_map/reduce_scatter | solution.py:270
  1033.6 118.8 %reduce-scatter.21.cloned.1.call-start = ((), (), s32[]{:S(2)}) async-start(), calls=%async_computation.20 | async-start | bytes 3276800 | tf_op jit(solution)/shard_map/reduce_scatter | solution.py:270
  1033.6 73.0 %collective-permute-start.47 = (bf16[2560,640]{1,0:T(8,128)(2,1)S(1)}, bf16[2560,640]{1,0:T(8,128)(2,1)S(1)}, u32[]{:S(2)}, u32[]{:S(2)}) collective-permute-start(bf16[2560,640]{1,0:T(8,128)(2,1)S(1)} %copy-done.8), channel_id=1, source_target_pairs={{0,2},{1,3},{2,0},{3,1},{4,6},{5,7},{6,4},{7,5},{8,10},{9,11},{10,... | collective-permute-start | bytes 9830408 | tf_op jit(solution)/shard_map/ppermute | solution.py:206
  1116.6 75.0 %reduce-scatter.23.cloned.1.call-start = ((), (), s32[]{:S(2)}) async-start(), calls=%async_computation.21 | async-start | bytes 3276800 | tf_op jit(solution)/shard_map/reduce_scatter | solution.py:270
  1131.2 141.5 %all-gather.21.cloned.1.call-start = ((), (), s32[]{:S(2)}) async-start(), calls=%async_computation.22 | async-start | bytes 6553600 | tf_op jit(solution)/shard_map/all_gather | solution.py:276
  (57 other events, 1493.5 us)
Sparse Core Ops, SparseCore 0:
  34.1 58.8 all-gather.8
  100.9 41.7 all-gather.10
  231.9 62.2 all-gather.12
  440.0 35.6 reduce-scatter.8
  478.5 35.8 reduce-scatter.10
  544.6 35.6 reduce-scatter.12
  583.2 35.7 reduce-scatter.14
  622.8 57.5 all-gather.14
  688.3 40.3 all-gather.16
  816.6 62.2 all-gather.18
  1019.5 35.6 reduce-scatter.16
  1058.5 35.7 reduce-scatter.18
  1116.7 35.6 reduce-scatter.20
  1155.8 35.7 reduce-scatter.22
  1215.5 57.2 all-gather.20
where the time goes:
time: 1290 us; the launch traced here: 1280 us
  waiting for transfers between devices  903 us (70%)
  Pallas kernels  167 us (13%)
  matrix products  68.1 us (5%)
  local copies, waits for them, and re-layouts  57.4 us (4%)
  starting transfers between devices  44.4 us (3%)
  blocking collectives  16.6 us (1%)
  between operations  14.7 us (1%)
  other arithmetic  13.2 us (1%)
    ppermute x52, waiting for transfers between devices, swap(): return lax.ppermute(value, axis, [(i, i ^ bits) for i in range(4)])  687 us
    reduce_scatter x8, waiting for transfers between devices, layers(): lax.psum_scatter(jnp.dot(ffn_in, w, preferred_element_type=jnp.float32),...  120 us
    pallas_call x2, Pallas kernels, ffn_up(): pl.pallas_call(ffn_up_kernel, grid=(n_cols // block,), in_specs=[pl.Block...  83.8 us
    dot_general x8, matrix products, layers(): jnp.dot(ffn_in, w, preferred_element_type=jnp.float32)  68.1 us
    all_gather x1, waiting for transfers between devices, layers(): full = lax.all_gather(ordered, 'heads', axis=1, tiled=True)  49.5 us
    all_gather x2, waiting for transfers between devices, layers(): h_full = lax.all_gather(normed, 'heads', axis=0, tiled=True)  46.5 us
    ppermute x52, starting transfers between devices, swap(): return lax.ppermute(value, axis, [(i, i ^ bits) for i in range(4)])  42.6 us
    pallas_call x4, Pallas kernels, project(): pl.pallas_call(kernel, grid=(n_tok // Q_ROWS,), in_specs=[pl.BlockSpec((Q...  31.4 us
  transfers between devices with their start and end apart: 67, of which 37 were waited for; matrix products, arithmetic and copies ran while one was open for 7% of the time, Pallas kernels for 3%

commit v1 on v0

--- a/solution.py
+++ b/solution.py
@@ -1,3 +1,5 @@
+import functools
+
 import jax
 import jax.numpy as jnp
 from jax import lax
@@ -127,31 +129,170 @@
     )(bounds, q_loc, kv_all, kv_all, low)
 
 
-def ffn_up_kernel(h_ref, g0, g1, g2, g3, u0, u1, u2, u3, out_ref):
-    def chunk(i, _):
-        rows = pl.ds(pl.multiple_of(i * 256, 256), 256)
-        h_rows = h_ref.at[rows, :]
-        gate = dot4(h_rows, (g0, g1, g2, g3)).astype(jnp.bfloat16).astype(jnp.float32)
-        up = dot4(h_rows, (u0, u1, u2, u3)).astype(jnp.bfloat16).astype(jnp.float32)
-        out_ref[rows, :] = (jax.nn.gelu(gate, approximate=True) * up).astype(jnp.bfloat16)
+FFN_ROWS = 256
+FFN_COLS = 512
+
+
+def ffn_kernel(make_next, h_ref, g0, g1, g2, g3, u0, u1, u2, u3, d0, d1, d2, d3, mid_ref, post_ref, next_ref, hidden_ref, hnext_ref,
+               wg, wu, wd, h_buf, m_buf, send, own, recv, load_sem, wd_sem, h_sem, io_sem, send_sem, recv_sem):
+    head = lax.axis_index('heads')
+    y_pos, z_pos = head % 2, head // 2
+    over_y = head + 1 - 2 * y_pos
+    over_z = head + 2 - 4 * z_pos
+    diag = over_y + 2 - 4 * z_pos
+    chunks = (diag, over_y, over_z, head)
+    depth = g0.shape[0]
+    width = wg.shape[0]
+    half = width // 2
+    n_blocks = width // FFN_COLS
+
+    def load_h(c):
+        rows = pl.ds(pl.multiple_of(chunks[c] * FFN_ROWS, FFN_ROWS), FFN_ROWS)
+        return pltpu.make_async_copy(h_ref.at[rows, :], h_buf.at[c % 2], h_sem.at[c % 2])
+
+    def load_up(n):
+        copies = []
+        for j, (g, u) in enumerate(((g0, u0), (g1, u1), (g2, u2), (g3, u3))):
+            cols = pl.ds(n * FFN_COLS, FFN_COLS)
+            rows = pl.ds(j * depth, depth)
+            copies.append(pltpu.make_async_copy(g.at[:, cols], wg.at[rows, cols], load_sem.at[n, j]))
+            copies.append(pltpu.make_async_copy(u.at[:, cols], wu.at[rows, cols], load_sem.at[n, 4 + j]))
+        return copies
+
+    load_h(0).start()
+    for n in range(n_blocks):
+        for copy in load_up(n):
+            copy.start()
+    down = [pltpu.make_async_copy(d, wd.at[:, pl.ds(j * depth, depth)], wd_sem.at[j]) for j, d in enumerate((d0, d1, d2, d3))]
+    for copy in down:
+        copy.start()
+
+    barrier = pltpu.get_barrier_semaphore()
+    for peer in (over_y, over_z):
+        pl.semaphore_signal(barrier, inc=1, device_id={'heads': peer}, device_id_type=pl.DeviceIdType.MESH)
+    pl.semaphore_wait(barrier, 2)
+
+    def up_block(c, cols):
+        h = h_buf[c % 2]
+        gate = jnp.dot(h, wg[:, cols], preferred_element_type=jnp.float32).astype(jnp.bfloat16).astype(jnp.float32)
+        up = jnp.dot(h, wu[:, cols], preferred_element_type=jnp.float32).astype(jnp.bfloat16).astype(jnp.float32)
+        m_buf[:, cols] = (jax.nn.gelu(gate, approximate=True) * up).astype(jnp.bfloat16)
+
+    def up_chunk(c):
+        load_h(c).wait()
+        if c < 3:
+            load_h(c + 1).start()
+        if c == 0:
+            for n in range(n_blocks):
+                for copy in load_up(n):
+                    copy.wait()
+                up_block(c, slice(n * FFN_COLS, (n + 1) * FFN_COLS))
+        else:
+            def step(n, _):
+                up_block(c, pl.ds(pl.multiple_of(n * FFN_COLS, FFN_COLS), FFN_COLS))
+                return 0
+
+            lax.fori_loop(0, n_blocks, step, 0)
+
+    def down_half(dst, side):
+        def step(n, _):
+            cols = pl.ds(pl.multiple_of(n * 256, 256), 256)
+            wcols = pl.ds(pl.multiple_of(side * half + n * 256, 256), 256)
+            dst[:, cols] = jnp.dot(m_buf[...], wd[:, wcols], preferred_element_type=jnp.float32)
+            return 0
+
+        lax.fori_loop(0, half // 256, step, 0)
+
+    def move(k, peer):
+        return pltpu.make_async_remote_copy(src_ref=send.at[k], dst_ref=recv.at[k], send_sem=send_sem.at[k], recv_sem=recv_sem.at[k],
+                                            device_id={'heads': peer}, device_id_type=pl.DeviceIdType.MESH)
+
+    def add_received(k, got):
+        def step(i, _):
+            rows = pl.ds(pl.multiple_of(i * 32, 32), 32)
+            send[k, rows, :] = send[k, rows, :] + recv[got, rows, :]
+            return 0
+
+        lax.fori_loop(0, FFN_ROWS // 32, step, 0)
+
+    sends = [move(0, over_y), move(1, over_z), move(2, over_y), move(3, over_z), move(4, over_z), move(5, over_y)]
+    up_chunk(0)
+    for copy in down:
+        copy.wait()
+    down_half(send.at[0], 0)
+    sends[0].start()
+    down_half(send.at[1], 1)
+    sends[1].start()
+    up_chunk(1)
+    down_half(send.at[2], 0)
+    sends[2].start()
+    down_half(send.at[5], 1)
+    up_chunk(2)
+    down_half(send.at[3], 1)
+    sends[3].start()
+    down_half(send.at[4], 0)
+    sends[0].wait_recv()
+    add_received(4, 0)
+    sends[4].start()
+    sends[1].wait_recv()
+    add_received(5, 1)
+    sends[5].start()
+    up_chunk(3)
+    mid_load = pltpu.make_async_copy(mid_ref, h_buf.at[0], io_sem.at[0])
+    mid_load.start()
+    down_half(own.at[0], 0)
+    down_half(own.at[1], 1)
+    mid_load.wait()
+    for k in range(2, 6):
+        sends[k].wait_recv()
+
+    def finish(i, _):
+        rows = pl.ds(pl.multiple_of(i * 32, 32), 32)
+        a = own[0, rows, :] + recv[2, rows, :] + recv[4, rows, :]
+        b = own[1, rows, :] + recv[3, rows, :] + recv[5, rows, :]
+        ffn = jnp.concatenate([a, b], axis=1).astype(jnp.bfloat16).astype(jnp.float32)
+        hidden = (h_buf[0, rows, :].astype(jnp.float32) + norm_rows(ffn, post_ref[...])).astype(jnp.bfloat16)
+        m_buf[rows, :] = hidden
+        if make_next:
+            h_buf[1, rows, :] = norm_rows(hidden.astype(jnp.float32), next_ref[...]).astype(jnp.bfloat16)
         return 0
 
-    lax.fori_loop(0, h_ref.shape[0] // 256, chunk, 0)
-
-
-def ffn_up(h_full, gates, ups):
+    lax.fori_loop(0, FFN_ROWS // 32, finish, 0)
+    outs = [pltpu.make_async_copy(m_buf, hidden_ref, io_sem.at[1])]
+    if make_next:
+        outs.append(pltpu.make_async_copy(h_buf.at[1], hnext_ref, io_sem.at[2]))
+    for copy in outs:
+        copy.start()
+    for k in range(6):
+        sends[k].wait_send()
+    for copy in outs:
+        copy.wait()
+
+
+def ffn_last_kernel(*refs):
+    ffn_kernel(False, *refs[:17], None, *refs[17:])
+
+
+def ffn(h_full, gates, ups, downs, mid, post, nxt, layer):
     n_tok, width = h_full.shape
-    depth, n_cols = gates[0].shape
-    block = 512
+    rows = mid.shape[0]
+    hbm = pl.BlockSpec(memory_space=pl.ANY)
+    vmem = pl.BlockSpec(memory_space=pltpu.VMEM)
+    n_out = 2 if layer == 0 else 1
     return pl.pallas_call(
-        ffn_up_kernel,
-        grid=(n_cols // block,),
-        in_specs=[pl.BlockSpec((n_tok, width), lambda n: (0, 0))] + [pl.BlockSpec((depth, block), lambda n: (0, n))] * 8,
-        out_specs=pl.BlockSpec((n_tok, block), lambda n: (0, n)),
-        out_shape=jax.ShapeDtypeStruct((n_tok, n_cols), jnp.bfloat16),
-        compiler_params=pltpu.CompilerParams(dimension_semantics=("arbitrary",)),
-        cost_estimate=pl.CostEstimate(flops=4 * n_tok * width * n_cols, bytes_accessed=40_000_000, transcendentals=n_tok * n_cols),
-    )(h_full, *gates, *ups)
+        functools.partial(ffn_kernel, True) if layer == 0 else ffn_last_kernel,
+        in_specs=[hbm] * 14 + [vmem] * 2,
+        out_specs=[hbm] * n_out,
+        out_shape=[jax.ShapeDtypeStruct((rows, width), jnp.bfloat16)] * n_out,
+        scratch_shapes=[pltpu.VMEM((width, width), jnp.bfloat16)] * 3
+        + [pltpu.VMEM((2, FFN_ROWS, width), jnp.bfloat16), pltpu.VMEM((FFN_ROWS, width), jnp.bfloat16),
+           pltpu.VMEM((6, FFN_ROWS, width // 2), jnp.float32), pltpu.VMEM((2, FFN_ROWS, width // 2), jnp.float32),
+           pltpu.VMEM((6, FFN_ROWS, width // 2), jnp.float32),
+           pltpu.SemaphoreType.DMA((width // FFN_COLS, 8)), pltpu.SemaphoreType.DMA((4,)), pltpu.SemaphoreType.DMA((2,)),
+           pltpu.SemaphoreType.DMA((3,)), pltpu.SemaphoreType.DMA((6,)), pltpu.SemaphoreType.DMA((6,))],
+        compiler_params=pltpu.CompilerParams(collective_id=layer, has_side_effects=True, vmem_limit_bytes=67043328),
+        cost_estimate=pl.CostEstimate(flops=6 * n_tok * width * width, bytes_accessed=50_000_000, transcendentals=n_tok * width),
+    )(h_full, *gates, *ups, *downs, mid, post, nxt)
 
 
 def pre_kernel(x0, x1, x2, x3, scale_ref, hidden_ref, h_ref):
@@ -160,12 +301,13 @@
     h_ref[...] = norm_rows(hidden.astype(jnp.float32), scale_ref[...]).astype(jnp.bfloat16)
 
 
-def out_kernel(o0, o1, o2, o3, a0, a1, a2, a3, b0, b1, b2, b3, resid_ref, post_ref, next_ref, mid_ref, h2_ref):
+def out_kernel(o0, o1, o2, o3, a0, a1, a2, a3, a4, b0, b1, b2, b3, b4, resid_ref, post_ref, next_ref, mid_ref, h2_ref):
     half = a0.shape[1] // 2
+    depth = o3.shape[1] // 2
     near, far = None, None
-    for o, a, b in zip((o0, o1, o2, o3), (a0, a1, a2, a3), (b0, b1, b2, b3)):
-        part_a = jnp.dot(o[...], a[...], preferred_element_type=jnp.float32)
-        part_b = jnp.dot(o[...], b[...], preferred_element_type=jnp.float32)
+    for o, a, b in zip((o0[...], o1[...], o2[...], o3[:, :depth], o3[:, depth:]), (a0, a1, a2, a3, a4), (b0, b1, b2, b3, b4)):
+        part_a = jnp.dot(o, a[...], preferred_element_type=jnp.float32)
+        part_b = jnp.dot(o, b[...], preferred_element_type=jnp.float32)
         near = part_a if near is None else near + part_a
         far = part_b if far is None else far + part_b
     attn = jnp.concatenate([near[:, :half], far[:, :half], near[:, half:], far[:, half:]], axis=1)
@@ -175,21 +317,14 @@
     h2_ref[...] = norm_rows(mid.astype(jnp.float32), next_ref[...]).astype(jnp.bfloat16)
 
 
-def post_kernel(f0, f1, f2, f3, mid_ref, post_ref, next_ref, hidden_ref, h_ref):
-    ffn = jnp.concatenate([f0[...], f1[...], f2[...], f3[...]], axis=1).astype(jnp.bfloat16).astype(jnp.float32)
-    hidden = (mid_ref[...].astype(jnp.float32) + norm_rows(ffn, post_ref[...])).astype(jnp.bfloat16)
-    hidden_ref[...] = hidden
-    h_ref[...] = norm_rows(hidden.astype(jnp.float32), next_ref[...]).astype(jnp.bfloat16)
-
-
-def whole(kernel, n_out, rows, width, flops, *args):
+def whole(kernel, n_out, rows, width, flops, fixed, *args):
     blk = 128
     full = lambda v: pl.BlockSpec(v.shape, lambda i: (0, 0))
     tiled = lambda v: pl.BlockSpec((blk, v.shape[1]), lambda i: (i, 0))
     return pl.pallas_call(
         kernel,
         grid=(rows // blk,),
-        in_specs=[tiled(v) if v.shape[0] == rows else full(v) for v in args],
+        in_specs=[tiled(v) if v.shape[0] == rows and k not in fixed else full(v) for k, v in enumerate(args)],
         out_specs=[pl.BlockSpec((blk, width), lambda i: (i, 0))] * n_out,
         out_shape=[jax.ShapeDtypeStruct((rows, width), jnp.bfloat16)] * n_out,
         compiler_params=pltpu.CompilerParams(dimension_semantics=("arbitrary",)),
@@ -215,8 +350,10 @@
         both = jnp.concatenate([own, swap(own, 2)], axis=-1)
         y = swap(both, 1, 'heads')
         z = swap(both, 2, 'heads')
-        d = swap(y, 2, 'heads')
-        a = (both, y, z, d)
+        half = both.shape[0] // 2
+        d0 = swap(y[:half], 2, 'heads')
+        d1 = swap(z[half:], 1, 'heads')
+        a = (both, y, z, d0, d1)
         b = tuple(swap(v, 1) for v in a)
         return a, b
 
@@ -228,8 +365,7 @@
         rows_m = n_tok // 4
         rows_own = n_tok // 16
 
-        scales_all = lax.all_gather(norm_scales, 'model')
-        scales = jnp.concatenate([lax.dynamic_index_in_dim(scales_all, me ^ j, 0, keepdims=False) for j in range(4)], axis=-1)
+        scales = jnp.concatenate([norm_scales] + [swap(norm_scales, j) for j in range(1, 4)], axis=-1)
         row = lambda l, i: scales[l, i:i + 1]
 
         xs = [lax.dynamic_slice(hidden_in, ((me ^ j) * rows_m + head * rows_own, 0), (rows_own, part)) for j in range(4)]
@@ -245,7 +381,7 @@
             pieces.append((gather_pieces(w_qkv[l]), gather_out(w_out[l]),
                            gather_pieces(w_gate[l]), gather_pieces(w_up[l]), gather_pieces(w_down[l])))
 
-        hidden, normed = whole(pre_kernel, 2, rows_own, width, 100_000_000, *xs, row(0, 0))
+        hidden, normed = whole(pre_kernel, 2, rows_own, width, 100_000_000, (), *xs, row(0, 0))
 
         settings = ((GLOBAL_BASE, GLOBAL_FACTOR, n_tok), (LOCAL_BASE, 1.0, WINDOW))
         kv_list = []
@@ -264,11 +400,10 @@
             o_loc = attend(q_loc, kv_all, low[:, None], bounds)
             os = [lax.dynamic_slice(o_loc, ((head ^ j) * rows_own, 0), (rows_own, 512)) for j in range(4)]
             os = [os[0]] + [swap(os[j], j, 'heads') for j in range(1, 4)]
-            mid, normed2 = whole(out_kernel, 2, rows_own, width, 2 * rows_own * 2048 * width, *os, *out_a, *out_b, hidden, row(l, 1), row(l, 2))
+            mid, normed2 = whole(out_kernel, 2, rows_own, width, 2 * rows_own * 2048 * width, range(4, 14), *os, *out_a, *out_b, hidden, row(l, 1), row(l, 2))
             h2_full = lax.all_gather(normed2, 'heads', axis=0, tiled=True)
-            ffn_in = ffn_up(h2_full, gate_p, up_p)
-            f_parts = [lax.psum_scatter(jnp.dot(ffn_in, w, preferred_element_type=jnp.float32), 'heads', scatter_dimension=0, tiled=True) for w in down_p]
-            hidden, normed = whole(post_kernel, 2, rows_own, width, 100_000_000, *f_parts, mid, row(l, 3), row(1, 0))
+            outs = ffn(h2_full, gate_p, up_p, down_p, mid, row(l, 3), row(1, 0), l)
+            hidden, normed = outs if l == 0 else (outs[0], None)
 
         mine = [hidden[:, :part]] + [swap(hidden[:, j * part:(j + 1) * part], j) for j in range(1, 4)]
         stacked = jnp.stack(mine)

time: 1290 us -> 1160 us (0.90)
  waiting for transfers between devices: 903 us -> 706 us
  Pallas kernels: 167 us -> 309 us
  matrix products: 68.1 us -> 0 us
  blocking collectives: 16.6 us -> 0 us
    pallas_call x2, Pallas kernels: 83.8 us -> 233 us  [ffn(): pl.pallas_call(functools.partial(ffn_kernel, True) if layer == 0 else ffn...]
    reduce_scatter x8 -> x0, waiting for transfers between devices: 120 us -> none  [layers(): lax.psum_scatter(jnp.dot(ffn_in, w, preferred_element_type=jnp.float32),...]
    ppermute x52 -> x59, waiting for transfers between devices: 687 us -> 612 us  [swap(): return lax.ppermute(value, axis, [(i, i ^ bits) for i in range(4)])]
    dot_general x8 -> x0, matrix products: 68.1 us -> none  [layers(): jnp.dot(ffn_in, w, preferred_element_type=jnp.float32)]
    all_gather x1 -> x0, blocking collectives: 16.6 us -> none  [layers(): scales_all = lax.all_gather(norm_scales, 'model')]
    pallas_call x5 -> x3, Pallas kernels: 29.7 us -> 22.4 us  [whole(): pl.pallas_call(kernel, grid=(rows // blk,), in_specs=[tiled(v) if v.shape...]
    ppermute x52 -> x59, starting transfers between devices: 42.6 us -> 47.5 us  [swap(): return lax.ppermute(value, axis, [(i, i ^ bits) for i in range(4)])]
    unnamed x79 -> x92, local copies, waits for them, and re-layouts: 25.9 us -> 23.8 us
  transfers between devices with their start and end apart: 67 -> 66, of which waited for: 37 -> 28; matrix products, arithmetic and copies ran while one was open for 7% -> 4% of each run, Pallas kernels for 3% -> 4%
where the time goes in v1:
time: 1160 us
  waiting for transfers between devices  706 us (61%)
  Pallas kernels  309 us (27%)
  local copies, waits for them, and re-layouts  62.2 us (5%)
  starting transfers between devices  48 us (4%)
  other arithmetic  15 us (1%)
  between operations  14.9 us (1%)
    ppermute x59, waiting for transfers between devices, swap(): return lax.ppermute(value, axis, [(i, i ^ bits) for i in range(4)])  612 us
    pallas_call x2, Pallas kernels, ffn(): pl.pallas_call(functools.partial(ffn_kernel, True) if layer == 0 else ffn...  233 us
    all_gather x1, waiting for transfers between devices, layers(): full = lax.all_gather(ordered, 'heads', axis=1, tiled=True)  49.1 us
    ppermute x59, starting transfers between devices, swap(): return lax.ppermute(value, axis, [(i, i ^ bits) for i in range(4)])  47.5 us
    all_gather x2, waiting for transfers between devices, layers(): h_full = lax.all_gather(normed, 'heads', axis=0, tiled=True)  45.4 us
    pallas_call x4, Pallas kernels, project(): pl.pallas_call(kernel, grid=(n_tok // Q_ROWS,), in_specs=[pl.BlockSpec((Q...  31.6 us
    unnamed x92, local copies, waits for them, and re-layouts  23.8 us
  transfers between devices with their start and end apart: 66, of which 28 were waited for; matrix products, arithmetic and copies ran while one was open for 4% of the time, Pallas kernels for 4%

profile of v1, /device:TPU:0, one launch (start us, length us, event | category | flops | bytes accessed | tf_op | source)
XLA Modules:
  0.0 1155.6 jit_solution(13588438273050582023)
XLA Ops:
  8.0 2.5 collective-permute-start.4
  15.7 7.8 collective-permute-done.1.x2
  23.5 5.9 collective-permute-done.2.x3
  30.1 2.9 shard_map.130
  37.4 29.2 %collective-permute-done.7.w2 = bf16[640,1024]{1,0:T(8,128)(2,1)S(1)} collective-permute-done((bf16[640,1024]{1,0:T(8,128)(2,1)S(1)}, bf16[640,1024]{1,0:T(8,128)(2,1)S(1)}, u32[]{:S(2)}, u32[]{:S(2)}) %collective-permute-start.7) | collective-permute-done | bytes 1310752 | tf_op jit(solution)/shard_map/ppermute | solution.py:341
  67.9 3.1 multiply_sine_fusion.1
  71.0 21.2 %all-gather.8.cloned.1.call-done.h_ref = bf16[1024,2560]{1,0:T(8,128)(2,1)} async-done(((bf16[256,2560]{1,0:T(8,128)(2,1)}), bf16[1024,2560]{1,0:T(8,128)(2,1)}) %all-gather.8.cloned.1.call-update) | async-done | bytes 5242896 | tf_op jit(solution)/shard_map/all_gather | solution.py:392
  92.2 7.8 shard_map.132
  100.0 2.2 slice_bitcast_fusion.12
  103.7 26.2 %collective-permute-done.12 = bf16[512,640]{1,0:T(8,128)(2,1)S(1)} collective-permute-done((bf16[512,640]{1,0:T(8,128)(2,1)S(1)}, bf16[512,640]{1,0:T(8,128)(2,1)S(1)}, u32[]{:S(2)}, u32[]{:S(2)}) %collective-permute-start.12) | collective-permute-done | bytes 655392 | tf_op jit(solution)/shard_map/ppermute | solution.py:341
  131.4 25.5 %collective-permute-done.13.a1 = bf16[512,1280]{1,0:T(8,128)(2,1)S(1)} collective-permute-done((bf16[512,1280]{1,0:T(8,128)(2,1)S(1)}, bf16[512,1280]{1,0:T(8,128)(2,1)S(1)}, u32[]{:S(2)}, u32[]{:S(2)}) %collective-permute-start.13) | collective-permute-done | bytes 1310752 | tf_op jit(solution)/shard_map/ppermute | solution.py:341
  158.4 2.8 collective-permute-done.14.a2
  166.1 6.2 collective-permute-done.15.a3
  174.1 7.9 shard_map.131.q_ref
  182.0 11.2 shard_map.133
  198.7 5.1 slice_bitcast_fusion.2
  205.6 4.6 collective-permute-start.23
  210.9 9.7 shard_map.134
  220.9 5.0 slice_bitcast_fusion.1
  225.9 3.2 collective-permute-start.26
  229.2 5.7 slice_bitcast_fusion
  236.7 45.3 %collective-permute-done.23.g2 = bf16[640,2560]{1,0:T(8,128)(2,1)} collective-permute-done((bf16[640,2560]{1,0:T(8,128)(2,1)S(1)}, bf16[640,2560]{1,0:T(8,128)(2,1)}, u32[]{:S(2)}, u32[]{:S(2)}) %collective-permute-start.23) | collective-permute-done | bytes 3276832 | tf_op jit(solution)/shard_map/ppermute | solution.py:341
  282.0 70.1 %collective-permute-done.26.u2 = bf16[640,2560]{1,0:T(8,128)(2,1)S(1)} collective-permute-done((bf16[640,2560]{1,0:T(8,128)(2,1)S(1)}, bf16[640,2560]{1,0:T(8,128)(2,1)S(1)}, u32[]{:S(2)}, u32[]{:S(2)}) %collective-permute-start.26) | collective-permute-done | bytes 3276832 | tf_op jit(solution)/shard_map/ppermute | solution.py:341
  352.1 70.0 %collective-permute-done.29.d2 = bf16[2560,640]{1,0:T(8,128)(2,1)S(1)} collective-permute-done((bf16[2560,640]{1,0:T(8,128)(2,1)S(1)}, bf16[2560,640]{1,0:T(8,128)(2,1)S(1)}, u32[]{:S(2)}, u32[]{:S(2)}) %collective-permute-start.29) | collective-permute-done | bytes 3276832 | tf_op jit(solution)/shard_map/ppermute | solution.py:341
  428.7 116.6 %shard_map.135 = (bf16[256,2560]{1,0:T(8,128)(2,1)}, bf16[256,2560]{1,0:T(8,128)(2,1)}) custom-call(bf16[1024,2560]{1,0:T(8,128)(2,1)} %all-gather.12.cloned.1.call-done.h_ref, bf16[640,2560]{1,0:T(8,128)(2,1)} %copy-done.8, bf16[640,2560]{1,0:T(8,128)(2,1)} %collective-permute-done.22.g1, bf16[640,2560]{1,0:T(8,128)(2,1)} %collective-permute-done.23.g2, ...), custom_call_target="tpu_custom_call" | custom-call | flops 40265318400 | bytes 50000000 | tf_op jit(solution)/shard_map/pallas_call | solution.py:282
  546.9 28.7 %collective-permute-done.32.w2 = bf16[640,1024]{1,0:T(8,128)(2,1)S(1)} collective-permute-done((bf16[640,1024]{1,0:T(8,128)(2,1)}, bf16[640,1024]{1,0:T(8,128)(2,1)S(1)}, u32[]{:S(2)}, u32[]{:S(2)}) %collective-permute-start.32) | collective-permute-done | bytes 1310752 | tf_op jit(solution)/shard_map/ppermute | solution.py:341
  575.7 3.8 multiply_sine_fusion
  579.4 24.2 %all-gather.14.cloned.1.call-done.h_ref = bf16[1024,2560]{1,0:T(8,128)(2,1)} async-done(((bf16[256,2560]{1,0:T(8,128)(2,1)}), bf16[1024,2560]{1,0:T(8,128)(2,1)}) %all-gather.14.cloned.1.call-update) | async-done | bytes 5242896 | tf_op jit(solution)/shard_map/all_gather | solution.py:392
  603.6 7.8 shard_map.137
  613.0 24.0 %collective-permute-done.37 = bf16[512,640]{1,0:T(8,128)(2,1)S(1)} collective-permute-done((bf16[512,640]{1,0:T(8,128)(2,1)S(1)}, bf16[512,640]{1,0:T(8,128)(2,1)S(1)}, u32[]{:S(2)}, u32[]{:S(2)}) %collective-permute-start.37) | collective-permute-done | bytes 655392 | tf_op jit(solution)/shard_map/ppermute | solution.py:341
  638.5 25.5 %collective-permute-done.38.a1 = bf16[512,1280]{1,0:T(8,128)(2,1)S(1)} collective-permute-done((bf16[512,1280]{1,0:T(8,128)(2,1)S(1)}, bf16[512,1280]{1,0:T(8,128)(2,1)S(1)}, u32[]{:S(2)}, u32[]{:S(2)}) %collective-permute-start.38) | collective-permute-done | bytes 1310752 | tf_op jit(solution)/shard_map/ppermute | solution.py:341
  671.5 7.8 collective-permute-done.40.a3
  680.7 8.1 shard_map.136.q_ref
  688.8 11.2 shard_map.138
  705.5 4.0 collective-permute-done.34.o1
  711.3 3.9 collective-permute-done.36.o3
  715.9 9.8 shard_map.139
  727.9 4.0 collective-permute-start.48
  734.5 69.2 %collective-permute-done.48.refs_3_ = bf16[640,2560]{1,0:T(8,128)(2,1)S(1)} collective-permute-done((bf16[640,2560]{1,0:T(8,128)(2,1)S(1)}, bf16[640,2560]{1,0:T(8,128)(2,1)S(1)}, u32[]{:S(2)}, u32[]{:S(2)}) %collective-permute-start.48) | collective-permute-done | bytes 3276832 | tf_op jit(solution)/shard_map/ppermute | solution.py:341
  805.4 68.5 %collective-permute-done.51.refs_7_ = bf16[640,2560]{1,0:T(8,128)(2,1)S(1)} collective-permute-done((bf16[640,2560]{1,0:T(8,128)(2,1)}, bf16[640,2560]{1,0:T(8,128)(2,1)S(1)}, u32[]{:S(2)}, u32[]{:S(2)}) %collective-permute-start.51) | collective-permute-done | bytes 3276832 | tf_op jit(solution)/shard_map/ppermute | solution.py:341
  873.9 70.0 %collective-permute-done.54.refs_11_ = bf16[2560,640]{1,0:T(8,128)(2,1)S(1)} collective-permute-done((bf16[2560,640]{1,0:T(8,128)(2,1)}, bf16[2560,640]{1,0:T(8,128)(2,1)S(1)}, u32[]{:S(2)}, u32[]{:S(2)}) %collective-permute-start.54) | collective-permute-done | bytes 3276832 | tf_op jit(solution)/shard_map/ppermute | solution.py:341
  950.3 116.0 %shard_map.140 = bf16[256,2560]{1,0:T(8,128)(2,1)} custom-call(bf16[1024,2560]{1,0:T(8,128)(2,1)} %all-gather.18.cloned.1.call-done.refs_0_, bf16[640,2560]{1,0:T(8,128)(2,1)} %get-tuple-element.31.refs_1_, bf16[640,2560]{1,0:T(8,128)(2,1)} %copy-done.29, bf16[640,2560]{1,0:T(8,128)(2,1)} %copy-done.30, bf16[640,2560]{1,0:T(8,128)(2,1)} %copy-done.40, ...), custom_call_target="tpu_custom_call" | custom-call | flops 40265318400 | bytes 50000000 | tf_op jit(solution)/shard_map/pallas_call | solution.py:282
  1069.7 8.0 collective-permute-done.58
  1077.7 7.2 collective-permute-done.57
  1086.4 2.6 slice_bitcast_fusion.7
  1090.2 4.0 maximum_bitcast_fusion
  1094.1 49.1 %all-gather.20.cloned.1.call-done = bf16[4,1024,640]{2,1,0:T(8,128)(2,1)} async-done(((bf16[4,256,640]{2,1,0:T(8,128)(2,1)}), bf16[4,1024,640]{2,1,0:T(8,128)(2,1)}) %all-gather.20.cloned.1.call-update) | async-done | bytes 5242896 | tf_op jit(solution)/shard_map/all_gather | solution.py:411
  1143.2 5.3 copy.26
  (232 shorter events, 80.2 us)
Async XLA Ops:
  7.2 85.0 %all-gather.8.cloned.1.call-start = ((), (), s32[]{:S(2)}) async-start(), calls=%async_computation | async-start | bytes 6553600 | tf_op jit(solution)/shard_map/all_gather | solution.py:392
  14.9 14.5 %collective-permute-start.2 = (bf16[256,640]{1,0:T(8,128)(2,1)S(1)}, bf16[256,640]{1,0:T(8,128)(2,1)S(1)}, u32[]{:S(2)}, u32[]{:S(2)}) collective-permute-start(bf16[256,640]{1,0:T(8,128)(2,1)S(1)} %get-tuple-element.33), channel_id=1, source_target_pairs={{0,3},{1,2},{2,1},{3,0},{4,7},{5,6},{6,5},{7,4},{8,11},{9,10},{10,... | collective-permute-start | bytes 983048 | tf_op jit(solution)/shard_map/ppermute | solution.py:341
  33.1 149.0 %all-gather.10.cloned.1.call-start = ((), (), s32[]{:S(2)}) async-start(), calls=%async_computation.1 | async-start | bytes 5242880 | tf_op jit(solution)/shard_map/all_gather | solution.py:394
  35.5 31.1 %collective-permute-start.7 = (bf16[640,1024]{1,0:T(8,128)(2,1)S(1)}, bf16[640,1024]{1,0:T(8,128)(2,1)S(1)}, u32[]{:S(2)}, u32[]{:S(2)}) collective-permute-start(bf16[640,1024]{1,0:T(8,128)(2,1)S(1)} %get-tuple-element.42.w0), channel_id=1, source_target_pairs={{0,2},{1,3},{2,0},{3,1},{4,6},{5,7},{6,4},{7,5},{8,10},{9,11},{10,... | collective-permute-start | bytes 3932168 | tf_op jit(solution)/shard_map/ppermute | solution.py:341
  37.1 33.9 %collective-permute-start.6 = (bf16[640,1024]{1,0:T(8,128)(2,1)S(1)}, bf16[640,1024]{1,0:T(8,128)(2,1)}, u32[]{:S(2)}, u32[]{:S(2)}) collective-permute-start(bf16[640,1024]{1,0:T(8,128)(2,1)S(1)} %get-tuple-element.42.w0), channel_id=1, source_target_pairs={{0,1},{1,0},{2,3},{3,2},{4,5},{5,4},{6,7},{7,6},{8,9},{9,8},{10,11... | collective-permute-start | bytes 3932168 | tf_op jit(solution)/shard_map/ppermute | solution.py:341
  100.0 328.7 %all-gather.12.cloned.1.call-start = ((), (), s32[]{:S(2)}) async-start(), calls=%async_computation.2 | async-start | bytes 6553600 | tf_op jit(solution)/shard_map/all_gather | solution.py:404
  102.3 27.6 %collective-permute-start.12 = (bf16[512,640]{1,0:T(8,128)(2,1)S(1)}, bf16[512,640]{1,0:T(8,128)(2,1)S(1)}, u32[]{:S(2)}, u32[]{:S(2)}) collective-permute-start(bf16[512,640]{1,0:T(8,128)(2,1)S(1)} %get-tuple-element.52), channel_id=1, source_target_pairs={{0,2},{1,3},{2,0},{3,1},{4,6},{5,7},{6,4},{7,5},{8,10},{9,11},{10,... | collective-permute-start | bytes 1966088 | tf_op jit(solution)/shard_map/ppermute | solution.py:341
  130.0 26.9 %collective-permute-start.13 = (bf16[512,1280]{1,0:T(8,128)(2,1)S(1)}, bf16[512,1280]{1,0:T(8,128)(2,1)S(1)}, u32[]{:S(2)}, u32[]{:S(2)}) collective-permute-start(bf16[512,1280]{1,0:T(8,128)(2,1)S(1)} %pad_maximum_fusion.a0), channel_id=1, source_target_pairs={{0,4},{4,0},{8,12},{12,8},{1,5},{5,1},{9,13},{13,9},{2,6},{6,2},{1... | collective-permute-start | bytes 3932168 | tf_op jit(solution)/shard_map/ppermute | solution.py:341
  131.4 29.8 %collective-permute-start.14 = (bf16[512,1280]{1,0:T(8,128)(2,1)S(1)}, bf16[512,1280]{1,0:T(8,128)(2,1)}, u32[]{:S(2)}, u32[]{:S(2)}) collective-permute-start(bf16[512,1280]{1,0:T(8,128)(2,1)S(1)} %pad_maximum_fusion.a0), channel_id=1, source_target_pairs={{0,8},{4,12},{8,0},{12,4},{1,9},{5,13},{9,1},{13,5},{2,10},{6,14},... | collective-permute-start | bytes 3932168 | tf_op jit(solution)/shard_map/ppermute | solution.py:341
  157.0 15.3 %collective-permute-start.15 = (bf16[256,1280]{1,0:T(8,128)(2,1)S(1)}, bf16[256,1280]{1,0:T(8,128)(2,1)}, u32[]{:S(2)}, u32[]{:S(2)}) collective-permute-start(bf16[256,1280]{1,0:T(8,128)(2,1)S(1)} %slice.147), channel_id=1, source_target_pairs={{0,8},{4,12},{8,0},{12,4},{1,9},{5,13},{9,1},{13,5},{2,10},{6,14},... | collective-permute-start | bytes 1966088 | tf_op jit(solution)/shard_map/ppermute | solution.py:341
  163.2 32.1 %collective-permute-start.17 = (bf16[512,1280]{1,0:T(8,128)(2,1)S(1)}, bf16[512,1280]{1,0:T(8,128)(2,1)}, u32[]{:S(2)}, u32[]{:S(2)}) collective-permute-start(bf16[512,1280]{1,0:T(8,128)(2,1)S(1)} %pad_maximum_fusion.a0), channel_id=1, source_target_pairs={{0,1},{1,0},{2,3},{3,2},{4,5},{5,4},{6,7},{7,6},{8,9},{9,8},{10,11... | collective-permute-start | bytes 3932168 | tf_op jit(solution)/shard_map/ppermute | solution.py:341
  163.2 32.1 %collective-permute-start.18 = (bf16[512,1280]{1,0:T(8,128)(2,1)S(1)}, bf16[512,1280]{1,0:T(8,128)(2,1)}, u32[]{:S(2)}, u32[]{:S(2)}) collective-permute-start(bf16[512,1280]{1,0:T(8,128)(2,1)S(1)} %collective-permute-done.13.a1), channel_id=1, source_target_pairs={{0,1},{1,0},{2,3},{3,2},{4,5},{5,4},{6,7},{7,6},{8,9},{9,8},{10,11... | collective-permute-start | bytes 3932168 | tf_op jit(solution)/shard_map/ppermute | solution.py:341
  163.7 33.5 %collective-permute-start.19 = (bf16[512,1280]{1,0:T(8,128)(2,1)}, bf16[512,1280]{1,0:T(8,128)(2,1)}, u32[]{:S(2)}, u32[]{:S(2)}) collective-permute-start(bf16[512,1280]{1,0:T(8,128)(2,1)} %collective-permute-done.14.a2), channel_id=1, source_target_pairs={{0,1},{1,0},{2,3},{3,2},{4,5},{5,4},{6,7},{7,6},{8,9},{9,8},{10,11... | collective-permute-start | bytes 3932168 | tf_op jit(solution)/shard_map/ppermute | solution.py:341
  172.2 31.6 %collective-permute-start.20 = (bf16[256,1280]{1,0:T(8,128)(2,1)}, bf16[256,1280]{1,0:T(8,128)(2,1)}, u32[]{:S(2)}, u32[]{:S(2)}) collective-permute-start(bf16[256,1280]{1,0:T(8,128)(2,1)} %collective-permute-done.15.a3), channel_id=1, source_target_pairs={{0,1},{1,0},{2,3},{3,2},{4,5},{5,4},{6,7},{7,6},{8,9},{9,8},{10,11... | collective-permute-start | bytes 1966088 | tf_op jit(solution)/shard_map/ppermute | solution.py:341
  174.1 31.5 %collective-permute-start.21 = (bf16[256,1280]{1,0:T(8,128)(2,1)}, bf16[256,1280]{1,0:T(8,128)(2,1)}, u32[]{:S(2)}, u32[]{:S(2)}) collective-permute-start(bf16[256,1280]{1,0:T(8,128)(2,1)} %collective-permute-done.16.a4), channel_id=1, source_target_pairs={{0,1},{1,0},{2,3},{3,2},{4,5},{5,4},{6,7},{7,6},{8,9},{9,8},{10,11... | collective-permute-start | bytes 1966088 | tf_op jit(solution)/shard_map/ppermute | solution.py:341
  195.3 14.9 %collective-permute-start.9 = (bf16[256,512]{1,0:T(8,128)(2,1)S(1)}, bf16[256,512]{1,0:T(8,128)(2,1)S(1)}, u32[]{:S(2)}, u32[]{:S(2)}) collective-permute-start(bf16[256,512]{1,0:T(8,128)(2,1)S(1)} %get-tuple-element.59), channel_id=1, source_target_pairs={{0,4},{4,0},{8,12},{12,8},{1,5},{5,1},{9,13},{13,9},{2,6},{6,2},{1... | collective-permute-start | bytes 786440 | tf_op jit(solution)/shard_map/ppermute | solution.py:341
  195.3 14.9 %collective-permute-start.10 = (bf16[256,512]{1,0:T(8,128)(2,1)S(1)}, bf16[256,512]{1,0:T(8,128)(2,1)}, u32[]{:S(2)}, u32[]{:S(2)}) collective-permute-start(bf16[256,512]{1,0:T(8,128)(2,1)S(1)} %get-tuple-element.58), channel_id=1, source_target_pairs={{0,8},{4,12},{8,0},{12,4},{1,9},{5,13},{9,1},{13,5},{2,10},{6,14},... | collective-permute-start | bytes 786440 | tf_op jit(solution)/shard_map/ppermute | solution.py:341
  203.8 32.4 %collective-permute-start.22 = (bf16[640,2560]{1,0:T(8,128)(2,1)S(1)}, bf16[640,2560]{1,0:T(8,128)(2,1)}, u32[]{:S(2)}, u32[]{:S(2)}) collective-permute-start(bf16[640,2560]{1,0:T(8,128)(2,1)S(1)} %get-tuple-element.32.g0), channel_id=1, source_target_pairs={{0,1},{1,0},{2,3},{3,2},{4,5},{5,4},{6,7},{7,6},{8,9},{9,8},{10,11... | collective-permute-start | bytes 9830408 | tf_op jit(solution)/shard_map/ppermute | solution.py:341
  205.6 76.4 %collective-permute-start.23 = (bf16[640,2560]{1,0:T(8,128)(2,1)S(1)}, bf16[640,2560]{1,0:T(8,128)(2,1)}, u32[]{:S(2)}, u32[]{:S(2)}) collective-permute-start(bf16[640,2560]{1,0:T(8,128)(2,1)S(1)} %get-tuple-element.32.g0), channel_id=1, source_target_pairs={{0,2},{1,3},{2,0},{3,1},{4,6},{5,7},{6,4},{7,5},{8,10},{9,11},{10,... | collective-permute-start | bytes 9830408 | tf_op jit(solution)/shard_map/ppermute | solution.py:341
  220.6 383.0 %all-gather.14.cloned.1.call-start = ((), (), s32[]{:S(2)}) async-start(), calls=%async_computation.3 | async-start | bytes 6553600 | tf_op jit(solution)/shard_map/all_gather | solution.py:392
  225.9 126.2 %collective-permute-start.26 = (bf16[640,2560]{1,0:T(8,128)(2,1)S(1)}, bf16[640,2560]{1,0:T(8,128)(2,1)S(1)}, u32[]{:S(2)}, u32[]{:S(2)}) collective-permute-start(bf16[640,2560]{1,0:T(8,128)(2,1)S(1)} %get-tuple-element.30.u0), channel_id=1, source_target_pairs={{0,2},{1,3},{2,0},{3,1},{4,6},{5,7},{6,4},{7,5},{8,10},{9,11},{10,... | collective-permute-start | bytes 9830408 | tf_op jit(solution)/shard_map/ppermute | solution.py:341
  234.8 187.3 %collective-permute-start.29 = (bf16[2560,640]{1,0:T(8,128)(2,1)S(1)}, bf16[2560,640]{1,0:T(8,128)(2,1)S(1)}, u32[]{:S(2)}, u32[]{:S(2)}) collective-permute-start(bf16[2560,640]{1,0:T(8,128)(2,1)S(1)} %get-tuple-element.28.d0), channel_id=1, source_target_pairs={{0,2},{1,3},{2,0},{3,1},{4,6},{5,7},{6,4},{7,5},{8,10},{9,11},{10,... | collective-permute-start | bytes 9830408 | tf_op jit(solution)/shard_map/ppermute | solution.py:341
  236.2 185.9 %collective-permute-start.25 = (bf16[640,2560]{1,0:T(8,128)(2,1)S(1)}, bf16[640,2560]{1,0:T(8,128)(2,1)S(1)}, u32[]{:S(2)}, u32[]{:S(2)}) collective-permute-start(bf16[640,2560]{1,0:T(8,128)(2,1)S(1)} %get-tuple-element.30.u0), channel_id=1, source_target_pairs={{0,1},{1,0},{2,3},{3,2},{4,5},{5,4},{6,7},{7,6},{8,9},{9,8},{10,11... | collective-permute-start | bytes 9830408 | tf_op jit(solution)/shard_map/ppermute | solution.py:341
  236.2 185.9 %collective-permute-start.28 = (bf16[2560,640]{1,0:T(8,128)(2,1)S(1)}, bf16[2560,640]{1,0:T(8,128)(2,1)S(1)}, u32[]{:S(2)}, u32[]{:S(2)}) collective-permute-start(bf16[2560,640]{1,0:T(8,128)(2,1)S(1)} %get-tuple-element.28.d0), channel_id=1, source_target_pairs={{0,1},{1,0},{2,3},{3,2},{4,5},{5,4},{6,7},{7,6},{8,9},{9,8},{10,11... | collective-permute-start | bytes 9830408 | tf_op jit(solution)/shard_map/ppermute | solution.py:341
  282.0 140.2 %collective-permute-start.24 = (bf16[640,2560]{1,0:T(8,128)(2,1)}, bf16[640,2560]{1,0:T(8,128)(2,1)S(1)}, u32[]{:S(2)}, u32[]{:S(2)}) collective-permute-start(bf16[640,2560]{1,0:T(8,128)(2,1)} %collective-permute-done.23.g2), channel_id=1, source_target_pairs={{0,1},{1,0},{2,3},{3,2},{4,5},{5,4},{6,7},{7,6},{8,9},{9,8},{10,11... | collective-permute-start | bytes 9830408 | tf_op jit(solution)/shard_map/ppermute | solution.py:341
  352.1 70.1 %collective-permute-start.27 = (bf16[640,2560]{1,0:T(8,128)(2,1)S(1)}, bf16[640,2560]{1,0:T(8,128)(2,1)S(1)}, u32[]{:S(2)}, u32[]{:S(2)}) collective-permute-start(bf16[640,2560]{1,0:T(8,128)(2,1)S(1)} %collective-permute-done.26.u2), channel_id=1, source_target_pairs={{0,1},{1,0},{2,3},{3,2},{4,5},{5,4},{6,7},{7,6},{8,9},{9,8},{10,11... | collective-permute-start | bytes 9830408 | tf_op jit(solution)/shard_map/ppermute | solution.py:341
  545.4 143.5 %all-gather.16.cloned.1.call-start = ((), (), s32[]{:S(2)}) async-start(), calls=%async_computation.4 | async-start | bytes 5242880 | tf_op jit(solution)/shard_map/all_gather | solution.py:394
  545.4 30.2 %collective-permute-start.32 = (bf16[640,1024]{1,0:T(8,128)(2,1)}, bf16[640,1024]{1,0:T(8,128)(2,1)S(1)}, u32[]{:S(2)}, u32[]{:S(2)}) collective-permute-start(bf16[640,1024]{1,0:T(8,128)(2,1)} %get-tuple-element.41.w0), channel_id=1, source_target_pairs={{0,2},{1,3},{2,0},{3,1},{4,6},{5,7},{6,4},{7,5},{8,10},{9,11},{10,... | collective-permute-start | bytes 3932168 | tf_op jit(solution)/shard_map/ppermute | solution.py:341
  546.9 32.5 %collective-permute-start.31 = (bf16[640,1024]{1,0:T(8,128)(2,1)}, bf16[640,1024]{1,0:T(8,128)(2,1)S(1)}, u32[]{:S(2)}, u32[]{:S(2)}) collective-permute-start(bf16[640,1024]{1,0:T(8,128)(2,1)} %get-tuple-element.41.w0), channel_id=1, source_target_pairs={{0,1},{1,0},{2,3},{3,2},{4,5},{5,4},{6,7},{7,6},{8,9},{9,8},{10,11... | collective-permute-start | bytes 3932168 | tf_op jit(solution)/shard_map/ppermute | solution.py:341
  611.5 338.9 %all-gather.18.cloned.1.call-start = ((), (), s32[]{:S(2)}) async-start(), calls=%async_computation.5 | async-start | bytes 6553600 | tf_op jit(solution)/shard_map/all_gather | solution.py:404
  611.5 25.5 %collective-permute-start.37 = (bf16[512,640]{1,0:T(8,128)(2,1)S(1)}, bf16[512,640]{1,0:T(8,128)(2,1)S(1)}, u32[]{:S(2)}, u32[]{:S(2)}) collective-permute-start(bf16[512,640]{1,0:T(8,128)(2,1)S(1)} %copy-done.13), channel_id=1, source_target_pairs={{0,2},{1,3},{2,0},{3,1},{4,6},{5,7},{6,4},{7,5},{8,10},{9,11},{10,... | collective-permute-start | bytes 1966088 | tf_op jit(solution)/shard_map/ppermute | solution.py:341
  637.2 26.9 %collective-permute-start.38 = (bf16[512,1280]{1,0:T(8,128)(2,1)S(1)}, bf16[512,1280]{1,0:T(8,128)(2,1)S(1)}, u32[]{:S(2)}, u32[]{:S(2)}) collective-permute-start(bf16[512,1280]{1,0:T(8,128)(2,1)S(1)} %pad_maximum_fusion.1.a0), channel_id=1, source_target_pairs={{0,4},{4,0},{8,12},{12,8},{1,5},{5,1},{9,13},{13,9},{2,6},{6,2},{1... | collective-permute-start | bytes 3932168 | tf_op jit(solution)/shard_map/ppermute | solution.py:341
  638.5 28.7 %collective-permute-start.39 = (bf16[512,1280]{1,0:T(8,128)(2,1)S(1)}, bf16[512,1280]{1,0:T(8,128)(2,1)}, u32[]{:S(2)}, u32[]{:S(2)}) collective-permute-start(bf16[512,1280]{1,0:T(8,128)(2,1)S(1)} %pad_maximum_fusion.1.a0), channel_id=1, source_target_pairs={{0,8},{4,12},{8,0},{12,4},{1,9},{5,13},{9,1},{13,5},{2,10},{6,14},... | collective-permute-start | bytes 3932168 | tf_op jit(solution)/shard_map/ppermute | solution.py:341
  669.2 32.8 %collective-permute-start.42 = (bf16[512,1280]{1,0:T(8,128)(2,1)S(1)}, bf16[512,1280]{1,0:T(8,128)(2,1)}, u32[]{:S(2)}, u32[]{:S(2)}) collective-permute-start(bf16[512,1280]{1,0:T(8,128)(2,1)S(1)} %pad_maximum_fusion.1.a0), channel_id=1, source_target_pairs={{0,1},{1,0},{2,3},{3,2},{4,5},{5,4},{6,7},{7,6},{8,9},{9,8},{10,11... | collective-permute-start | bytes 3932168 | tf_op jit(solution)/shard_map/ppermute | solution.py:341
  669.2 33.4 %collective-permute-start.43 = (bf16[512,1280]{1,0:T(8,128)(2,1)S(1)}, bf16[512,1280]{1,0:T(8,128)(2,1)}, u32[]{:S(2)}, u32[]{:S(2)}) collective-permute-start(bf16[512,1280]{1,0:T(8,128)(2,1)S(1)} %collective-permute-done.38.a1), channel_id=1, source_target_pairs={{0,1},{1,0},{2,3},{3,2},{4,5},{5,4},{6,7},{7,6},{8,9},{9,8},{10,11... | collective-permute-start | bytes 3932168 | tf_op jit(solution)/shard_map/ppermute | solution.py:341
  669.7 34.4 %collective-permute-start.44 = (bf16[512,1280]{1,0:T(8,128)(2,1)}, bf16[512,1280]{1,0:T(8,128)(2,1)}, u32[]{:S(2)}, u32[]{:S(2)}) collective-permute-start(bf16[512,1280]{1,0:T(8,128)(2,1)} %collective-permute-done.39.a2), channel_id=1, source_target_pairs={{0,1},{1,0},{2,3},{3,2},{4,5},{5,4},{6,7},{7,6},{8,9},{9,8},{10,11... | collective-permute-start | bytes 3932168 | tf_op jit(solution)/shard_map/ppermute | solution.py:341
  679.3 26.3 %collective-permute-start.45 = (bf16[256,1280]{1,0:T(8,128)(2,1)S(1)}, bf16[256,1280]{1,0:T(8,128)(2,1)}, u32[]{:S(2)}, u32[]{:S(2)}) collective-permute-start(bf16[256,1280]{1,0:T(8,128)(2,1)S(1)} %collective-permute-done.40.a3), channel_id=1, source_target_pairs={{0,1},{1,0},{2,3},{3,2},{4,5},{5,4},{6,7},{7,6},{8,9},{9,8},{10,11... | collective-permute-start | bytes 1966088 | tf_op jit(solution)/shard_map/ppermute | solution.py:341
  680.7 24.9 %collective-permute-start.46 = (bf16[256,1280]{1,0:T(8,128)(2,1)}, bf16[256,1280]{1,0:T(8,128)(2,1)}, u32[]{:S(2)}, u32[]{:S(2)}) collective-permute-start(bf16[256,1280]{1,0:T(8,128)(2,1)} %collective-permute-done.41.a4), channel_id=1, source_target_pairs={{0,1},{1,0},{2,3},{3,2},{4,5},{5,4},{6,7},{7,6},{8,9},{9,8},{10,11... | collective-permute-start | bytes 1966088 | tf_op jit(solution)/shard_map/ppermute | solution.py:341
  725.8 417.5 %all-gather.20.cloned.1.call-start = ((), (), s32[]{:S(2)}) async-start(), calls=%async_computation.6 | async-start | bytes 6553600 | tf_op jit(solution)/shard_map/all_gather | solution.py:411
  727.9 75.8 %collective-permute-start.48 = (bf16[640,2560]{1,0:T(8,128)(2,1)S(1)}, bf16[640,2560]{1,0:T(8,128)(2,1)S(1)}, u32[]{:S(2)}, u32[]{:S(2)}) collective-permute-start(bf16[640,2560]{1,0:T(8,128)(2,1)S(1)} %copy-done.7), channel_id=1, source_target_pairs={{0,2},{1,3},{2,0},{3,1},{4,6},{5,7},{6,4},{7,5},{8,10},{9,11},{10,... | collective-permute-start | bytes 9830408 | tf_op jit(solution)/shard_map/ppermute | solution.py:341
  732.0 142.0 %collective-permute-start.51 = (bf16[640,2560]{1,0:T(8,128)(2,1)}, bf16[640,2560]{1,0:T(8,128)(2,1)S(1)}, u32[]{:S(2)}, u32[]{:S(2)}) collective-permute-start(bf16[640,2560]{1,0:T(8,128)(2,1)} %get-tuple-element.29.refs_5_), channel_id=1, source_target_pairs={{0,2},{1,3},{2,0},{3,1},{4,6},{5,7},{6,4},{7,5},{8,10},{9,11},{10,... | collective-permute-start | bytes 9830408 | tf_op jit(solution)/shard_map/ppermute | solution.py:341
  732.0 211.9 %collective-permute-start.54 = (bf16[2560,640]{1,0:T(8,128)(2,1)}, bf16[2560,640]{1,0:T(8,128)(2,1)S(1)}, u32[]{:S(2)}, u32[]{:S(2)}) collective-permute-start(bf16[2560,640]{1,0:T(8,128)(2,1)} %get-tuple-element.27.refs_9_), channel_id=1, source_target_pairs={{0,2},{1,3},{2,0},{3,1},{4,6},{5,7},{6,4},{7,5},{8,10},{9,11},{10,... | collective-permute-start | bytes 9830408 | tf_op jit(solution)/shard_map/ppermute | solution.py:341
  734.0 210.0 %collective-permute-start.50 = (bf16[640,2560]{1,0:T(8,128)(2,1)}, bf16[640,2560]{1,0:T(8,128)(2,1)S(1)}, u32[]{:S(2)}, u32[]{:S(2)}) collective-permute-start(bf16[640,2560]{1,0:T(8,128)(2,1)} %get-tuple-element.29.refs_5_), channel_id=1, source_target_pairs={{0,1},{1,0},{2,3},{3,2},{4,5},{5,4},{6,7},{7,6},{8,9},{9,8},{10,11... | collective-permute-start | bytes 9830408 | tf_op jit(solution)/shard_map/ppermute | solution.py:341
  734.0 210.0 %collective-permute-start.53 = (bf16[2560,640]{1,0:T(8,128)(2,1)}, bf16[2560,640]{1,0:T(8,128)(2,1)S(1)}, u32[]{:S(2)}, u32[]{:S(2)}) collective-permute-start(bf16[2560,640]{1,0:T(8,128)(2,1)} %get-tuple-element.27.refs_9_), channel_id=1, source_target_pairs={{0,1},{1,0},{2,3},{3,2},{4,5},{5,4},{6,7},{7,6},{8,9},{9,8},{10,11... | collective-permute-start | bytes 9830408 | tf_op jit(solution)/shard_map/ppermute | solution.py:341
  803.7 140.3 %collective-permute-start.49 = (bf16[640,2560]{1,0:T(8,128)(2,1)S(1)}, bf16[640,2560]{1,0:T(8,128)(2,1)S(1)}, u32[]{:S(2)}, u32[]{:S(2)}) collective-permute-start(bf16[640,2560]{1,0:T(8,128)(2,1)S(1)} %collective-permute-done.48.refs_3_), channel_id=1, source_target_pairs={{0,1},{1,0},{2,3},{3,2},{4,5},{5,4},{6,7},{7,6},{8,9},{9,8},{10,11... | collective-permute-start | bytes 9830408 | tf_op jit(solution)/shard_map/ppermute | solution.py:341
  873.9 70.1 %collective-permute-start.52 = (bf16[640,2560]{1,0:T(8,128)(2,1)S(1)}, bf16[640,2560]{1,0:T(8,128)(2,1)S(1)}, u32[]{:S(2)}, u32[]{:S(2)}) collective-permute-start(bf16[640,2560]{1,0:T(8,128)(2,1)S(1)} %collective-permute-done.51.refs_7_), channel_id=1, source_target_pairs={{0,1},{1,0},{2,3},{3,2},{4,5},{5,4},{6,7},{7,6},{8,9},{9,8},{10,11... | collective-permute-start | bytes 9830408 | tf_op jit(solution)/shard_map/ppermute | solution.py:341
  1068.1 16.7 %collective-permute-start.57 = (bf16[256,640]{1,0:T(8,128)(2,1)S(1)}, bf16[256,640]{1,0:T(8,128)(2,1)S(1)}, u32[]{:S(2)}, u32[]{:S(2)}) collective-permute-start(bf16[256,640]{1,0:T(8,128)(2,1)S(1)} %get-tuple-element.49), channel_id=1, source_target_pairs={{0,2},{1,3},{2,0},{3,1},{4,6},{5,7},{6,4},{7,5},{8,10},{9,11},{10,... | collective-permute-start | bytes 983048 | tf_op jit(solution)/shard_map/ppermute | solution.py:341
  1069.4 15.4 %collective-permute-start.56 = (bf16[256,640]{1,0:T(8,128)(2,1)S(1)}, bf16[256,640]{1,0:T(8,128)(2,1)S(1)}, u32[]{:S(2)}, u32[]{:S(2)}) collective-permute-start(bf16[256,640]{1,0:T(8,128)(2,1)S(1)} %get-tuple-element.50), channel_id=1, source_target_pairs={{0,1},{1,0},{2,3},{3,2},{4,5},{5,4},{6,7},{7,6},{8,9},{9,8},{10,11... | collective-permute-start | bytes 983048 | tf_op jit(solution)/shard_map/ppermute | solution.py:341
  (61 other events, 1112.1 us)
Sparse Core Ops, SparseCore 0:
  33.2 58.9 all-gather.7
  100.1 42.5 all-gather.9
  220.7 59.5 all-gather.11
  545.5 58.0 all-gather.13
  611.6 40.3 all-gather.15
  725.9 62.3 all-gather.17
  1086.6 56.6 all-gather.19

commit v2 on v1

--- a/solution.py
+++ b/solution.py
@@ -76,8 +76,24 @@
     )(h_full, *pieces, cos_tab, sin_tab, scale_row)
 
 
-def attention_kernel(bounds_ref, q_ref, k_ref, v_ref, low_ref, o_ref):
+def attention_kernel(layer, bounds_ref, q_ref, kv0, kv1, kv2, kv3, low_ref, *rest):
+    o_ref, key_ref, value_ref, kv_buf, in_sem, out_sem = rest[-6:]
     step = pl.program_id(0)
+    n_loc = kv0.shape[0]
+
+    @pl.when(step == 0)
+    def _():
+        copies = []
+        for j, piece in enumerate((kv0, kv1, kv2, kv3)):
+            rows = pl.ds(pl.multiple_of(bounds_ref[5 + j], 256), n_loc)
+            copies.append(pltpu.make_async_copy(piece, kv_buf.at[rows, :], in_sem.at[j]))
+        for copy in copies:
+            copy.start()
+        for copy in copies:
+            copy.wait()
+        pltpu.make_async_copy(kv_buf.at[:, pl.ds(0, HEAD_DIM)], key_ref.at[layer], out_sem.at[0]).start()
+        pltpu.make_async_copy(kv_buf.at[:, pl.ds(HEAD_DIM, HEAD_DIM)], value_ref.at[layer], out_sem.at[1]).start()
+
     row_base = bounds_ref[0] + step * Q_ROWS
     first_block = bounds_ref[1 + step] // KEY_BLOCK
     last_block = (row_base + Q_ROWS + KEY_BLOCK - 1) // KEY_BLOCK
@@ -90,8 +106,8 @@
     def one_block(block, carry):
         row_max, row_sum, acc = carry
         base = pl.multiple_of(block * KEY_BLOCK, KEY_BLOCK)
-        k_blk = k_ref[pl.ds(base, KEY_BLOCK), :]
-        v_blk = v_ref[pl.ds(base, KEY_BLOCK), :]
+        k_blk = kv_buf[pl.ds(base, KEY_BLOCK), :HEAD_DIM]
+        v_blk = kv_buf[pl.ds(base, KEY_BLOCK), HEAD_DIM:]
         scores = lax.dot_general(q2, k_blk, (((1,), (1,)), ((), ())), preferred_element_type=jnp.float32) * scale
         cols = base + lax.broadcasted_iota(jnp.int32, (1, KEY_BLOCK), 1)
         scores = jnp.where((cols >= low) & (cols <= rows), scores, MASKED)
@@ -109,37 +125,214 @@
     o_ref[:, :HEAD_DIM] = out[:Q_ROWS]
     o_ref[:, HEAD_DIM:] = out[Q_ROWS:]
 
-
-def attend(q_loc, kv_all, low, bounds):
+    @pl.when(step == pl.num_programs(0) - 1)
+    def _():
+        pltpu.make_async_copy(kv_buf.at[:, pl.ds(0, HEAD_DIM)], key_ref.at[layer], out_sem.at[0]).wait()
+        pltpu.make_async_copy(kv_buf.at[:, pl.ds(HEAD_DIM, HEAD_DIM)], value_ref.at[layer], out_sem.at[1]).wait()
+
+
+def attend(q_loc, kv_pieces, low, bounds, caches, layer):
     n_q = q_loc.shape[0]
-    n_tok = kv_all.shape[0]
+    n_tok = 4 * n_q
+    hbm = pl.BlockSpec(memory_space=pl.ANY)
+    cache = jax.ShapeDtypeStruct((2, n_tok, HEAD_DIM), jnp.bfloat16)
     return pl.pallas_call(
-        attention_kernel,
+        functools.partial(attention_kernel, layer),
         grid_spec=pltpu.PrefetchScalarGridSpec(
             num_scalar_prefetch=1,
             grid=(n_q // Q_ROWS,),
-            in_specs=[pl.BlockSpec((Q_ROWS, 512), lambda i, b: (i, 0)),
-                      pl.BlockSpec((n_tok, HEAD_DIM), lambda i, b: (0, 0)),
-                      pl.BlockSpec((n_tok, HEAD_DIM), lambda i, b: (0, 1)),
-                      pl.BlockSpec((Q_ROWS, 1), lambda i, b: (i, 0))],
-            out_specs=pl.BlockSpec((Q_ROWS, 512), lambda i, b: (i, 0))),
-        out_shape=jax.ShapeDtypeStruct((n_q, 512), jnp.bfloat16),
+            in_specs=[pl.BlockSpec((Q_ROWS, 512), lambda i, b: (i, 0))] + [hbm] * 4
+            + [pl.BlockSpec((Q_ROWS, 1), lambda i, b: (i, 0))] + [hbm] * len(caches),
+            out_specs=[pl.BlockSpec((Q_ROWS, 512), lambda i, b: (i, 0)), hbm, hbm],
+            scratch_shapes=[pltpu.VMEM((n_tok, 512), jnp.bfloat16), pltpu.SemaphoreType.DMA((4,)), pltpu.SemaphoreType.DMA((2,))]),
+        out_shape=[jax.ShapeDtypeStruct((n_q, 512), jnp.bfloat16), cache, cache],
+        input_output_aliases={7: 1, 8: 2} if caches else {},
         compiler_params=pltpu.CompilerParams(dimension_semantics=("arbitrary",)),
         cost_estimate=pl.CostEstimate(flops=2 * n_q * n_tok * 512, bytes_accessed=8_000_000, transcendentals=0),
-    )(bounds, q_loc, kv_all, kv_all, low)
+    )(bounds, q_loc, *kv_pieces, low, *caches)
+
+
+MESH = pl.DeviceIdType.MESH
+SPLIT = 128
+
+
+def head_peers():
+    head = lax.axis_index('heads')
+    over_y = head + 1 - 2 * (head % 2)
+    over_z = head + 2 - 4 * (head // 2)
+    return head, over_y, over_z, over_y + 2 - 4 * (head // 2)
+
+
+def meet(peers):
+    barrier = pltpu.get_barrier_semaphore()
+    for peer in peers:
+        pl.semaphore_signal(barrier, inc=1, device_id=peer, device_id_type=MESH)
+    pl.semaphore_wait(barrier, len(peers))
+
+
+def token_rows(head, part, base=0):
+    return pl.ds(pl.multiple_of(base + head * 2 * SPLIT + part * SPLIT, SPLIT), SPLIT)
+
+
+class HeadGather:
+    def __init__(self, src, full, local_sem, send_sem, recv_sem):
+        head, over_y, over_z, _ = head_peers()
+        self.local = [pltpu.make_async_copy(src.at[pl.ds(p * SPLIT, SPLIT), :], full.at[token_rows(head, p), :], local_sem.at[p]) for p in range(2)]
+
+        def remote(a, b, k, peer):
+            return pltpu.make_async_remote_copy(src_ref=a, dst_ref=b, send_sem=send_sem.at[k], recv_sem=recv_sem.at[k],
+                                                device_id={'heads': peer}, device_id_type=MESH)
+
+        mine = [(src.at[pl.ds(p * SPLIT, SPLIT), :], full.at[token_rows(head, p), :]) for p in range(2)]
+        self.y = [remote(*mine[p], p, over_y) for p in range(2)]
+        self.z = [remote(*mine[p], 2 + p, over_z) for p in range(2)]
+        top, low = full.at[token_rows(over_y, 0), :], full.at[token_rows(over_z, 1), :]
+        self.forward = [remote(top, top, 4, over_z), remote(low, low, 5, over_y)]
+
+    def start(self, p):
+        for copy in (self.y[p], self.z[p], self.local[p]):
+            copy.start()
+
+    def finish(self):
+        self.y[0].wait_recv()
+        self.forward[0].start()
+        self.z[1].wait_recv()
+        self.forward[1].start()
+        self.y[1].wait_recv()
+        self.z[0].wait_recv()
+        for copy in self.forward:
+            copy.wait_recv()
+        for copy in self.y + self.z + self.forward:
+            copy.wait_send()
+        for copy in self.local:
+            copy.wait()
+
+
+GATHER_SEMS = [pltpu.SemaphoreType.DMA((2,)), pltpu.SemaphoreType.DMA((6,)), pltpu.SemaphoreType.DMA((6,))]
+
+
+def pre_kernel(x0, x1, x2, x3, scale_ref, hidden_ref, full_ref, h_buf, local_sem, send_sem, recv_sem):
+    _, over_y, over_z, _ = head_peers()
+    meet([{'heads': over_y}, {'heads': over_z}])
+    gather = HeadGather(h_buf, full_ref, local_sem, send_sem, recv_sem)
+    for p in range(2):
+        def step(i, _):
+            rows = pl.ds(pl.multiple_of(p * SPLIT + i * 32, 32), 32)
+            hidden = jnp.concatenate([x0[rows, :], x1[rows, :], x2[rows, :], x3[rows, :]], axis=1)
+            hidden_ref[rows, :] = hidden
+            h_buf[rows, :] = norm_rows(hidden.astype(jnp.float32), scale_ref[...]).astype(jnp.bfloat16)
+            return 0
+
+        lax.fori_loop(0, SPLIT // 32, step, 0)
+        gather.start(p)
+    gather.finish()
+
+
+def first_norm(xs, scale):
+    rows, part = xs[0].shape
+    vmem = pl.BlockSpec(memory_space=pltpu.VMEM)
+    return pl.pallas_call(
+        pre_kernel,
+        in_specs=[vmem] * 5,
+        out_specs=[vmem, pl.BlockSpec(memory_space=pl.ANY)],
+        out_shape=[jax.ShapeDtypeStruct((rows, 4 * part), jnp.bfloat16), jax.ShapeDtypeStruct((4 * rows, 4 * part), jnp.bfloat16)],
+        scratch_shapes=[pltpu.VMEM((rows, 4 * part), jnp.bfloat16)] + GATHER_SEMS,
+        compiler_params=pltpu.CompilerParams(collective_id=2, has_side_effects=True),
+        cost_estimate=pl.CostEstimate(flops=500_000_000, bytes_accessed=8_000_000, transcendentals=0),
+        name="pre0",
+    )(*xs, scale)
+
+
+def out_kernel(o_ref, a0, a1, a2, a3, a4, b0, b1, b2, b3, b4, resid_ref, post_ref, next_ref, mid_ref, full_ref,
+               o_buf, w_buf, a_buf, h_buf, w_sem, o_sem, os_sem, or_sem, local_sem, send_sem, recv_sem):
+    head, over_y, over_z, diag = head_peers()
+    part = a0.shape[1] // 2
+    dim = o_ref.shape[1]
+    n_rows = 2 * SPLIT
+    loads = []
+    start = 0
+    for k, (a, b) in enumerate(((a0, b0), (a1, b1), (a2, b2), (a3, b3), (a4, b4))):
+        depth = a.shape[0]
+        for i, (src, col, dst) in enumerate(((a, 0, 0), (b, 0, 1), (a, 1, 2), (b, 1, 3))):
+            loads.append(pltpu.make_async_copy(src.at[:, pl.ds(col * part, part)], w_buf.at[pl.ds(start, depth), pl.ds(dst * part, part)], w_sem.at[k, i]))
+        start += depth
+
+    def rows_of(h):
+        return pl.ds(pl.multiple_of(h * n_rows, n_rows), n_rows)
+
+    own = pltpu.make_async_copy(o_ref.at[rows_of(head), :], o_buf.at[:, pl.ds(0, dim)], o_sem)
+    own.start()
+    for copy in loads:
+        copy.start()
+    meet([{'heads': over_y}, {'heads': over_z}, {'heads': diag}])
+    moves = [pltpu.make_async_remote_copy(src_ref=o_ref.at[rows_of(peer), :], dst_ref=o_buf.at[:, pl.ds(j * dim, dim)], send_sem=os_sem.at[j],
+                                          recv_sem=or_sem.at[j], device_id={'heads': peer}, device_id_type=MESH)
+             for j, peer in ((3, diag), (1, over_y), (2, over_z))]
+    for copy in moves:
+        copy.start()
+    own.wait()
+    for copy in loads:
+        copy.wait()
+    for copy in moves:
+        copy.wait_recv()
+    gather = HeadGather(h_buf, full_ref, local_sem, send_sem, recv_sem)
+    for p in range(2):
+        def project_block(n, _):
+            cols = pl.ds(pl.multiple_of(n * 512, 512), 512)
+            a_buf[:, cols] = jnp.dot(o_buf[p * SPLIT:(p + 1) * SPLIT, :], w_buf[:, cols], preferred_element_type=jnp.float32)
+            return 0
+
+        lax.fori_loop(0, w_buf.shape[1] // 512, project_block, 0)
+
+        def step(i, _):
+            rows = pl.ds(pl.multiple_of(i * 32, 32), 32)
+            all_rows = pl.ds(pl.multiple_of(p * SPLIT + i * 32, 32), 32)
+            attn = a_buf[rows, :].astype(jnp.bfloat16).astype(jnp.float32)
+            mid = (resid_ref[all_rows, :].astype(jnp.float32) + norm_rows(attn, post_ref[...])).astype(jnp.bfloat16)
+            mid_ref[all_rows, :] = mid
+            h_buf[all_rows, :] = norm_rows(mid.astype(jnp.float32), next_ref[...]).astype(jnp.bfloat16)
+            return 0
+
+        lax.fori_loop(0, SPLIT // 32, step, 0)
+        gather.start(p)
+    for copy in moves:
+        copy.wait_send()
+    gather.finish()
+
+
+def out_project(o_loc, out_a, out_b, resid, post, nxt, layer):
+    rows, width = resid.shape
+    n_tok, dim = o_loc.shape
+    hbm = pl.BlockSpec(memory_space=pl.ANY)
+    vmem = pl.BlockSpec(memory_space=pltpu.VMEM)
+    return pl.pallas_call(
+        out_kernel,
+        in_specs=[hbm] * 11 + [vmem] * 3,
+        out_specs=[vmem, hbm],
+        out_shape=[jax.ShapeDtypeStruct((rows, width), jnp.bfloat16), jax.ShapeDtypeStruct((n_tok, width), jnp.bfloat16)],
+        scratch_shapes=[pltpu.VMEM((rows, 4 * dim), jnp.bfloat16), pltpu.VMEM((4 * dim, width), jnp.bfloat16), pltpu.VMEM((SPLIT, width), jnp.float32),
+                        pltpu.VMEM((rows, width), jnp.bfloat16), pltpu.SemaphoreType.DMA((5, 4)), pltpu.SemaphoreType.DMA,
+                        pltpu.SemaphoreType.DMA((4,)), pltpu.SemaphoreType.DMA((4,))] + GATHER_SEMS,
+        compiler_params=pltpu.CompilerParams(collective_id=3 + layer, has_side_effects=True),
+        cost_estimate=pl.CostEstimate(flops=20_000_000_000, bytes_accessed=20_000_000, transcendentals=0),
+    )(o_loc, *out_a, *out_b, resid, post, nxt)
 
 
 FFN_ROWS = 256
 FFN_COLS = 512
 
 
-def ffn_kernel(make_next, h_ref, g0, g1, g2, g3, u0, u1, u2, u3, d0, d1, d2, d3, mid_ref, post_ref, next_ref, hidden_ref, hnext_ref,
-               wg, wu, wd, h_buf, m_buf, send, own, recv, load_sem, wd_sem, h_sem, io_sem, send_sem, recv_sem):
-    head = lax.axis_index('heads')
-    y_pos, z_pos = head % 2, head // 2
-    over_y = head + 1 - 2 * y_pos
-    over_z = head + 2 - 4 * z_pos
-    diag = over_y + 2 - 4 * z_pos
+def ffn_kernel(make_next, h_ref, g0, g1, g2, g3, u0, u1, u2, u3, d0, d1, d2, d3, mid_ref, post_ref, next_ref, hidden_ref, full_ref,
+               wg, wu, wd, h_buf, m_buf, send, own, recv, load_sem, wd_sem, h_sem, io_sem, send_sem, recv_sem, *gather_sems):
+    head, over_y, over_z, diag = head_peers()
+    peers = [{'heads': over_y}, {'heads': over_z}]
+    if not make_next:
+        me = lax.axis_index('model')
+        near = me + 1 - 2 * (me % 2)
+        far = me + 2 - 4 * (me // 2)
+        cross = near + 2 - 4 * (me // 2)
+        model_order = (me, near, far, cross)
+        peers += [{'model': peer} for peer in model_order[1:]]
     chunks = (diag, over_y, over_z, head)
     depth = g0.shape[0]
     width = wg.shape[0]
@@ -167,10 +360,7 @@
     for copy in down:
         copy.start()
 
-    barrier = pltpu.get_barrier_semaphore()
-    for peer in (over_y, over_z):
-        pl.semaphore_signal(barrier, inc=1, device_id={'heads': peer}, device_id_type=pl.DeviceIdType.MESH)
-    pl.semaphore_wait(barrier, 2)
+    meet(peers)
 
     def up_block(c, cols):
         h = h_buf[c % 2]
@@ -257,16 +447,68 @@
             h_buf[1, rows, :] = norm_rows(hidden.astype(jnp.float32), next_ref[...]).astype(jnp.bfloat16)
         return 0
 
-    lax.fori_loop(0, FFN_ROWS // 32, finish, 0)
-    outs = [pltpu.make_async_copy(m_buf, hidden_ref, io_sem.at[1])]
     if make_next:
-        outs.append(pltpu.make_async_copy(h_buf.at[1], hnext_ref, io_sem.at[2]))
-    for copy in outs:
+        gather = HeadGather(h_buf.at[1], full_ref, *gather_sems)
+        for p in range(2):
+            lax.fori_loop(p * SPLIT // 32, (p + 1) * SPLIT // 32, finish, 0)
+            gather.start(p)
+        store = pltpu.make_async_copy(m_buf, hidden_ref, io_sem.at[1])
+        store.start()
+        for k in range(6):
+            sends[k].wait_send()
+        gather.finish()
+        store.wait()
+    else:
+        lax.fori_loop(0, FFN_ROWS // 32, finish, 0)
+        spread(m_buf, hidden_ref, model_order, io_sem.at[1], *gather_sems)
+        for k in range(6):
+            sends[k].wait_send()
+
+
+def spread(src, out_ref, model_order, local_sem, model_send, model_recv, send_sem, recv_sem):
+    head, over_y, over_z, _ = head_peers()
+    part = out_ref.shape[1]
+    me = model_order[0]
+    rows_m = out_ref.shape[0] // 4
+
+    def block(owner, h):
+        return out_ref.at[pl.ds(pl.multiple_of(owner * rows_m + h * FFN_ROWS, FFN_ROWS), FFN_ROWS), :]
+
+    def half(owner, h, p):
+        return out_ref.at[token_rows(h, p, owner * rows_m), :]
+
+    def to_head(a, b, j, k, peer):
+        return pltpu.make_async_remote_copy(src_ref=a, dst_ref=b, send_sem=send_sem.at[j, k], recv_sem=recv_sem.at[j, k],
+                                            device_id={'heads': peer}, device_id_type=MESH)
+
+    local = pltpu.make_async_copy(src.at[:, pl.ds(0, part)], block(me, head), local_sem)
+    local.start()
+    across = {j: pltpu.make_async_remote_copy(src_ref=src.at[:, pl.ds(j * part, part)], dst_ref=block(me, head), send_sem=model_send.at[j],
+                                              recv_sem=model_recv.at[j], device_id={'model': model_order[j]}, device_id_type=MESH) for j in (1, 2, 3)}
+    for copy in across.values():
         copy.start()
-    for k in range(6):
-        sends[k].wait_send()
-    for copy in outs:
-        copy.wait()
+    first = []
+    for j, owner in enumerate(model_order):
+        if j:
+            across[j].wait_recv()
+        here = block(owner, head)
+        source = here if j else src.at[:, pl.ds(0, part)]
+        first.append((to_head(source, here, j, 0, over_y), to_head(source, here, j, 1, over_z)))
+        for copy in first[j]:
+            copy.start()
+    second = []
+    for j, owner in enumerate(model_order):
+        first[j][0].wait_recv()
+        second.append(to_head(half(owner, over_y, 0), half(owner, over_y, 0), j, 2, over_z))
+        second[-1].start()
+        first[j][1].wait_recv()
+        second.append(to_head(half(owner, over_z, 1), half(owner, over_z, 1), j, 3, over_y))
+        second[-1].start()
+    for copy in second:
+        copy.wait_recv()
+    for copy in second + [c for pair in first for c in pair] + list(across.values()):
+        copy.wait_send()
+    local.wait()
 
 
 def ffn_last_kernel(*refs):
@@ -278,58 +520,26 @@
     rows = mid.shape[0]
     hbm = pl.BlockSpec(memory_space=pl.ANY)
     vmem = pl.BlockSpec(memory_space=pltpu.VMEM)
-    n_out = 2 if layer == 0 else 1
+    if layer == 0:
+        outs = [jax.ShapeDtypeStruct((rows, width), jnp.bfloat16), jax.ShapeDtypeStruct((n_tok, width), jnp.bfloat16)]
+        sems = GATHER_SEMS
+    else:
+        outs = [jax.ShapeDtypeStruct((4 * n_tok, width // 4), jnp.bfloat16)]
+        sems = [pltpu.SemaphoreType.DMA((4,)), pltpu.SemaphoreType.DMA((4,)), pltpu.SemaphoreType.DMA((4, 4)), pltpu.SemaphoreType.DMA((4, 4))]
     return pl.pallas_call(
         functools.partial(ffn_kernel, True) if layer == 0 else ffn_last_kernel,
         in_specs=[hbm] * 14 + [vmem] * 2,
-        out_specs=[hbm] * n_out,
-        out_shape=[jax.ShapeDtypeStruct((rows, width), jnp.bfloat16)] * n_out,
+        out_specs=[hbm] * len(outs),
+        out_shape=outs,
         scratch_shapes=[pltpu.VMEM((width, width), jnp.bfloat16)] * 3
         + [pltpu.VMEM((2, FFN_ROWS, width), jnp.bfloat16), pltpu.VMEM((FFN_ROWS, width), jnp.bfloat16),
            pltpu.VMEM((6, FFN_ROWS, width // 2), jnp.float32), pltpu.VMEM((2, FFN_ROWS, width // 2), jnp.float32),
            pltpu.VMEM((6, FFN_ROWS, width // 2), jnp.float32),
            pltpu.SemaphoreType.DMA((width // FFN_COLS, 8)), pltpu.SemaphoreType.DMA((4,)), pltpu.SemaphoreType.DMA((2,)),
-           pltpu.SemaphoreType.DMA((3,)), pltpu.SemaphoreType.DMA((6,)), pltpu.SemaphoreType.DMA((6,))],
+           pltpu.SemaphoreType.DMA((3,)), pltpu.SemaphoreType.DMA((6,)), pltpu.SemaphoreType.DMA((6,))] + sems,
         compiler_params=pltpu.CompilerParams(collective_id=layer, has_side_effects=True, vmem_limit_bytes=67043328),
         cost_estimate=pl.CostEstimate(flops=6 * n_tok * width * width, bytes_accessed=50_000_000, transcendentals=n_tok * width),
     )(h_full, *gates, *ups, *downs, mid, post, nxt)
-
-
-def pre_kernel(x0, x1, x2, x3, scale_ref, hidden_ref, h_ref):
-    hidden = jnp.concatenate([x0[...], x1[...], x2[...], x3[...]], axis=1)
-    hidden_ref[...] = hidden
-    h_ref[...] = norm_rows(hidden.astype(jnp.float32), scale_ref[...]).astype(jnp.bfloat16)
-
-
-def out_kernel(o0, o1, o2, o3, a0, a1, a2, a3, a4, b0, b1, b2, b3, b4, resid_ref, post_ref, next_ref, mid_ref, h2_ref):
-    half = a0.shape[1] // 2
-    depth = o3.shape[1] // 2
-    near, far = None, None
-    for o, a, b in zip((o0[...], o1[...], o2[...], o3[:, :depth], o3[:, depth:]), (a0, a1, a2, a3, a4), (b0, b1, b2, b3, b4)):
-        part_a = jnp.dot(o, a[...], preferred_element_type=jnp.float32)
-        part_b = jnp.dot(o, b[...], preferred_element_type=jnp.float32)
-        near = part_a if near is None else near + part_a
-        far = part_b if far is None else far + part_b
-    attn = jnp.concatenate([near[:, :half], far[:, :half], near[:, half:], far[:, half:]], axis=1)
-    attn = attn.astype(jnp.bfloat16).astype(jnp.float32)
-    mid = (resid_ref[...].astype(jnp.float32) + norm_rows(attn, post_ref[...])).astype(jnp.bfloat16)
-    mid_ref[...] = mid
-    h2_ref[...] = norm_rows(mid.astype(jnp.float32), next_ref[...]).astype(jnp.bfloat16)
-
-
-def whole(kernel, n_out, rows, width, flops, fixed, *args):
-    blk = 128
-    full = lambda v: pl.BlockSpec(v.shape, lambda i: (0, 0))
-    tiled = lambda v: pl.BlockSpec((blk, v.shape[1]), lambda i: (i, 0))
-    return pl.pallas_call(
-        kernel,
-        grid=(rows // blk,),
-        in_specs=[tiled(v) if v.shape[0] == rows and k not in fixed else full(v) for k, v in enumerate(args)],
-        out_specs=[pl.BlockSpec((blk, width), lambda i: (i, 0))] * n_out,
-        out_shape=[jax.ShapeDtypeStruct((rows, width), jnp.bfloat16)] * n_out,
-        compiler_params=pltpu.CompilerParams(dimension_semantics=("arbitrary",)),
-        cost_estimate=pl.CostEstimate(flops=flops, bytes_accessed=8_000_000, transcendentals=0),
-    )(*args)
 
 
 def solution(mesh):
@@ -359,7 +569,6 @@
 
     def layers(hidden_in, seg_ids, positions, w_query, w_key, w_value, w_out, w_gate, w_up, w_down, norm_scales, qk_scales):
         n_tok, part = hidden_in.shape
-        width = part * 4
         me = lax.axis_index('model')
         head = lax.axis_index('heads')
         rows_m = n_tok // 4
@@ -381,38 +590,31 @@
             pieces.append((gather_pieces(w_qkv[l]), gather_out(w_out[l]),
                            gather_pieces(w_gate[l]), gather_pieces(w_up[l]), gather_pieces(w_down[l])))
 
-        hidden, normed = whole(pre_kernel, 2, rows_own, width, 100_000_000, (), *xs, row(0, 0))
+        hidden, h_full = first_norm(xs, row(0, 0))
 
         settings = ((GLOBAL_BASE, GLOBAL_FACTOR, n_tok), (LOCAL_BASE, 1.0, WINDOW))
-        kv_list = []
+        piece_rows = jnp.stack([(me ^ j) * rows_m for j in range(4)]).astype(jnp.int32)
+        tables = []
+        for rope_base, pos_factor, window in settings:
+            low = lax.dynamic_slice(jnp.maximum(starts, index - (window - 1)), (me * rows_m,), (rows_m,))
+            bounds = jnp.concatenate([piece_rows[:1], low[::Q_ROWS], piece_rows])
+            tables.append((*rope_tables(pos_loc, HEAD_DIM, rope_base, pos_factor), low[:, None], bounds))
+        caches = ()
         for l in range(2):
-            rope_base, pos_factor, window = settings[l]
             qkv_p, (out_a, out_b), gate_p, up_p, down_p = pieces[l]
-            cos_tab, sin_tab = rope_tables(pos_loc, HEAD_DIM, rope_base, pos_factor)
-            h_full = lax.all_gather(normed, 'heads', axis=0, tiled=True)
+            cos_tab, sin_tab, low, bounds = tables[l]
             kv_loc = project(kv_kernel, h_full, qkv_p, 1, cos_tab, sin_tab, qk_scales[l, 1:2])
-            kv_all = lax.all_gather(kv_loc, 'model', axis=0, tiled=True)
+            kv_pieces = gather_pieces(kv_loc)
             q_loc = project(q_kernel, h_full, qkv_p, 0, cos_tab, sin_tab, qk_scales[l, 0:1])
-            kv_list.append(kv_all)
-            low_all = jnp.maximum(starts, index - (window - 1))
-            low = lax.dynamic_slice(low_all, (me * rows_m,), (rows_m,))
-            bounds = jnp.concatenate([(me * rows_m).astype(jnp.int32)[None], low[::Q_ROWS]])
-            o_loc = attend(q_loc, kv_all, low[:, None], bounds)
-            os = [lax.dynamic_slice(o_loc, ((head ^ j) * rows_own, 0), (rows_own, 512)) for j in range(4)]
-            os = [os[0]] + [swap(os[j], j, 'heads') for j in range(1, 4)]
-            mid, normed2 = whole(out_kernel, 2, rows_own, width, 2 * rows_own * 2048 * width, range(4, 14), *os, *out_a, *out_b, hidden, row(l, 1), row(l, 2))
-            h2_full = lax.all_gather(normed2, 'heads', axis=0, tiled=True)
+            o_loc, *caches = attend(q_loc, kv_pieces, low, bounds, caches, l)
+            if l == 0:
+                o_loc, tables[1] = lax.optimization_barrier((o_loc, tables[1]))
+            mid, h2_full = out_project(o_loc, out_a, out_b, hidden, row(l, 1), row(l, 2), l)
             outs = ffn(h2_full, gate_p, up_p, down_p, mid, row(l, 3), row(1, 0), l)
-            hidden, normed = outs if l == 0 else (outs[0], None)
-
-        mine = [hidden[:, :part]] + [swap(hidden[:, j * part:(j + 1) * part], j) for j in range(1, 4)]
-        stacked = jnp.stack(mine)
-        ordered = jnp.stack([lax.dynamic_index_in_dim(stacked, me ^ j, 0, keepdims=False) for j in range(4)])
-        full = lax.all_gather(ordered, 'heads', axis=1, tiled=True)
-        hidden_out = full.reshape(n_tok, part)
-        keys = jnp.stack([kv[:, :HEAD_DIM] for kv in kv_list])[:, :, None, :]
-        values = jnp.stack([kv[:, HEAD_DIM:] for kv in kv_list])[:, :, None, :]
-        return hidden_out, keys, values
+            if l == 0:
+                hidden, h_full = outs
+
+        return outs[0], caches[0][:, :, None, :], caches[1][:, :, None, :]
 
     return jax.shard_map(layers, mesh=mesh,
                          in_specs=(P(None, 'model'), P(), P(), col_spec, col_spec, col_spec, row_spec, col_spec, col_spec, row_spec, P(None, None, 'model'), P()),

time: 1160 us -> 1000 us (0.86)
  waiting for transfers between devices: 706 us -> 357 us
  Pallas kernels: 309 us -> 559 us
  local copies, waits for them, and re-layouts: 62.2 us -> 34.2 us
  between operations: 14.9 us -> 1.48 us
    ppermute x59 -> x56, waiting for transfers between devices: 612 us -> 357 us  [swap(): return lax.ppermute(value, axis, [(i, i ^ bits) for i in range(4)])]
    pallas_call x5, Pallas kernels: 44.9 us -> 209 us  [the longest x2 135 us: out_project(): pl.pallas_call(out_kernel, in_specs=[hbm] * 11 + [vmem] * 3, out_specs=[v...]
    all_gather x7 -> x0, waiting for transfers between devices: 94.5 us -> none  [the longest x1 49.1 us: layers(): full = lax.all_gather(ordered, 'heads', axis=1, tiled=True)]
    pallas_call x2, Pallas kernels: 233 us -> 319 us  [ffn(): pl.pallas_call(functools.partial(ffn_kernel, True) if layer == 0 else ffn...]
    unnamed x92 -> x84, local copies, waits for them, and re-layouts: 23.8 us -> 10.8 us
    ppermute x59 -> x56, starting transfers between devices: 47.5 us -> 39.4 us  [swap(): return lax.ppermute(value, axis, [(i, i ^ bits) for i in range(4)])]
  transfers between devices with their start and end apart: 66 -> 56, of which waited for: 28 -> 16; matrix products, arithmetic and copies ran while one was open for 4% -> 3% of each run, Pallas kernels for 4% -> 40%
where the time goes in v2:
time: 1000 us; the launch traced here: 999 us
  Pallas kernels  559 us (56%)
  waiting for transfers between devices  357 us (36%)
  starting transfers between devices  39.4 us (4%)
  local copies, waits for them, and re-layouts  34.2 us (3%)
    ppermute x56, waiting for transfers between devices, swap(): return lax.ppermute(value, axis, [(i, i ^ bits) for i in range(4)])  357 us
    pallas_call x2, Pallas kernels, ffn(): pl.pallas_call(functools.partial(ffn_kernel, True) if layer == 0 else ffn...  319 us
    pallas_call x2, Pallas kernels, out_project(): pl.pallas_call(out_kernel, in_specs=[hbm] * 11 + [vmem] * 3, out_specs=[v...  135 us
    pallas_call x1, Pallas kernels, first_norm(): pl.pallas_call(pre_kernel, in_specs=[vmem] * 5, out_specs=[vmem, pl.Block...  49.7 us
    ppermute x56, starting transfers between devices, swap(): return lax.ppermute(value, axis, [(i, i ^ bits) for i in range(4)])  39.4 us
    pallas_call x4, Pallas kernels, project(): pl.pallas_call(kernel, grid=(n_tok // Q_ROWS,), in_specs=[pl.BlockSpec((Q...  31.4 us
    pallas_call x2, Pallas kernels, attend(): pl.pallas_call(functools.partial(attention_kernel, layer), grid_spec=pltp...  24.2 us
  transfers between devices with their start and end apart: 56, of which 16 were waited for; matrix products, arithmetic and copies ran while one was open for 3% of the time, Pallas kernels for 40%

profile of v2, /device:TPU:0, one launch (start us, length us, event | category | flops | bytes accessed | tf_op | source)
XLA Modules:
  0.0 999.1 jit_solution(8680377223029469503)
XLA Ops:
  1.4 2.5 collective-permute-start.4
  6.0 1.8 collective-permute-start.7
  10.0 2.1 constant_dynamic-slice_fusion
  14.3 44.4 %collective-permute-done.1.x2 = bf16[256,640]{1,0:T(8,128)(2,1)S(1)} collective-permute-done((bf16[256,640]{1,0:T(8,128)(2,1)S(1)}, bf16[256,640]{1,0:T(8,128)(2,1)S(1)}, u32[]{:S(2)}, u32[]{:S(2)}) %collective-permute-start.1) | collective-permute-done | bytes 327712 | tf_op jit(solution)/shard_map/ppermute | solution.py:551
  58.7 1.7 collective-permute-start.32
  60.5 4.5 collective-permute-done.2.x3
  65.7 1.6 collective-permute-start.37
  68.7 38.5 %collective-permute-done.37 = bf16[512,640]{1,0:T(8,128)(2,1)S(1)} collective-permute-done((bf16[512,640]{1,0:T(8,128)(2,1)S(1)}, bf16[512,640]{1,0:T(8,128)(2,1)S(1)}, u32[]{:S(2)}, u32[]{:S(2)}) %collective-permute-start.37) | collective-permute-done | bytes 655392 | tf_op jit(solution)/shard_map/ppermute | solution.py:551
  107.2 1.8 collective-permute-start.13
  109.0 1.6 collective-permute-start.14
  111.5 27.5 %collective-permute-done.13.a1 = bf16[512,1280]{1,0:T(8,128)(2,1)} collective-permute-done((bf16[512,1280]{1,0:T(8,128)(2,1)S(1)}, bf16[512,1280]{1,0:T(8,128)(2,1)}, u32[]{:S(2)}, u32[]{:S(2)}) %collective-permute-start.13) | collective-permute-done | bytes 1310752 | tf_op jit(solution)/shard_map/ppermute | solution.py:551
  139.0 1.8 collective-permute-done.14.a2
  143.8 21.7 %collective-permute-done.38.a1 = bf16[512,1280]{1,0:T(8,128)(2,1)S(1)} collective-permute-done((bf16[512,1280]{1,0:T(8,128)(2,1)S(1)}, bf16[512,1280]{1,0:T(8,128)(2,1)S(1)}, u32[]{:S(2)}, u32[]{:S(2)}) %collective-permute-start.38) | collective-permute-done | bytes 1310752 | tf_op jit(solution)/shard_map/ppermute | solution.py:551
  165.5 1.8 collective-permute-start.15
  167.3 1.5 collective-permute-start.16
  168.8 6.1 slice_bitcast_fusion.2
  176.2 1.5 collective-permute-start.23
  178.2 4.9 collective-permute-done.15.a3
  183.1 1.7 collective-permute-start.41
  184.9 3.1 slice_bitcast_fusion.1
  188.1 1.5 collective-permute-start.26
  189.6 5.4 collective-permute-done.40.a3
  197.3 2.2 slice_bitcast_fusion
  199.6 1.6 collective-permute-done.21.b4
  202.0 1.6 collective-permute-start.29
  204.8 3.5 multiply_sine_fusion.1
  208.3 42.1 %collective-permute-done.23.g2 = bf16[640,2560]{1,0:T(8,128)(2,1)} collective-permute-done((bf16[640,2560]{1,0:T(8,128)(2,1)}, bf16[640,2560]{1,0:T(8,128)(2,1)}, u32[]{:S(2)}, u32[]{:S(2)}) %collective-permute-start.23) | collective-permute-done | bytes 3276832 | tf_op jit(solution)/shard_map/ppermute | solution.py:551
  251.0 49.7 %pre0.1 = (bf16[256,2560]{1,0:T(8,128)(2,1)}, bf16[1024,2560]{1,0:T(8,128)(2,1)}) custom-call(bf16[256,640]{1,0:T(8,128)(2,1)} %get-tuple-element.57.x0, bf16[256,640]{1,0:T(8,128)(2,1)} %copy-done.32, bf16[256,640]{1,0:T(8,128)(2,1)} %copy-done.33, bf16[256,640]{1,0:T(8,128)(2,1)} %copy-done.34, f32[1,2560]{1,0:T(1,128)} %get-tuple-element.70.scale_ref), custom_call_target="tpu_custom_call" | custom-call | flops 500000000 | bytes 8000000 | tf_op jit(solution)/shard_map/pre0/pallas_call | solution.py:234
  300.8 7.8 shard_map.131.kv0
  308.6 12.0 %collective-permute-done.26.u2 = bf16[640,2560]{1,0:T(8,128)(2,1)} collective-permute-done((bf16[640,2560]{1,0:T(8,128)(2,1)}, bf16[640,2560]{1,0:T(8,128)(2,1)}, u32[]{:S(2)}, u32[]{:S(2)}) %collective-permute-start.26) | collective-permute-done | bytes 3276832 | tf_op jit(solution)/shard_map/ppermute | solution.py:551
  322.1 68.7 %collective-permute-done.29.d2 = bf16[2560,640]{1,0:T(8,128)(2,1)} collective-permute-done((bf16[2560,640]{1,0:T(8,128)(2,1)S(1)}, bf16[2560,640]{1,0:T(8,128)(2,1)}, u32[]{:S(2)}, u32[]{:S(2)}) %collective-permute-start.29) | collective-permute-done | bytes 3276832 | tf_op jit(solution)/shard_map/ppermute | solution.py:551
  390.8 19.6 %collective-permute-done.10.kv2 = bf16[1024,512]{1,0:T(8,128)(2,1)S(1)} collective-permute-done((bf16[1024,512]{1,0:T(8,128)(2,1)}, bf16[1024,512]{1,0:T(8,128)(2,1)S(1)}, u32[]{:S(2)}, u32[]{:S(2)}) %collective-permute-start.10) | collective-permute-done | bytes 1048608 | tf_op jit(solution)/shard_map/ppermute | solution.py:551
  412.4 3.1 multiply_sine_fusion
  419.0 7.9 shard_map.130.q_ref
  426.9 12.1 %shard_map.132 = (bf16[1024,512]{1,0:T(8,128)(2,1)}, bf16[2,4096,256]{2,1,0:T(8,128)(2,1)}, bf16[2,4096,256]{2,1,0:T(8,128)(2,1)}) custom-call(s32[9]{0:T(128)} %concatenate.20.bounds_ref, bf16[1024,512]{1,0:T(8,128)(2,1)} %shard_map.130.q_ref, bf16[1024,512]{1,0:T(8,128)(2,1)} %shard_map.131.kv0, bf16[1024,512]{1,0:T(8,128)(2,1)} %copy-done.22, ...), custom_call_target="tpu_custom_call" | custom-call | flops 4294967296 | bytes 8000000 | tf_op jit(solution)/shard_map/pallas_call | solution.py:139
  439.1 2.2 collective-permute-start.43
  441.3 65.8 %shard_map.133 = (bf16[256,2560]{1,0:T(8,128)(2,1)}, bf16[1024,2560]{1,0:T(8,128)(2,1)}) custom-call(bf16[1024,512]{1,0:T(8,128)(2,1)} %get-tuple-element.25.o_ref, bf16[512,1280]{1,0:T(8,128)(2,1)} %copy-done.10, bf16[512,1280]{1,0:T(8,128)(2,1)} %collective-permute-done.13.a1, bf16[512,1280]{1,0:T(8,128)(2,1)} %collective-permute-done.14.a2, ...), custom_call_target="tpu_custom_call" | custom-call | flops 20000000000 | bytes 20000000 | tf_op jit(solution)/shard_map/pallas_call | solution.py:308
  507.1 3.3 collective-permute-start.48
  510.5 2.0 collective-permute-start.54
  512.5 161.2 %shard_map.134 = (bf16[256,2560]{1,0:T(8,128)(2,1)}, bf16[1024,2560]{1,0:T(8,128)(2,1)}) custom-call(bf16[1024,2560]{1,0:T(8,128)(2,1)} %get-tuple-element.27.h_ref, bf16[640,2560]{1,0:T(8,128)(2,1)} %get-tuple-element.54.g0, bf16[640,2560]{1,0:T(8,128)(2,1)} %collective-permute-done.22.g1, bf16[640,2560]{1,0:T(8,128)(2,1)} %collective-permute-done.23.g2, ...), custom_call_target="tpu_custom_call" | custom-call | flops 40265318400 | bytes 50000000 | tf_op jit(solution)/shard_map/pallas_call | solution.py:529
  673.7 7.8 shard_map.136.kv0
  681.6 61.3 %collective-permute-done.35.kv2 = bf16[1024,512]{1,0:T(8,128)(2,1)S(1)} collective-permute-done((bf16[1024,512]{1,0:T(8,128)(2,1)}, bf16[1024,512]{1,0:T(8,128)(2,1)S(1)}, u32[]{:S(2)}, u32[]{:S(2)}) %collective-permute-start.35) | collective-permute-done | bytes 1048608 | tf_op jit(solution)/shard_map/ppermute | solution.py:551
  744.0 1.6 collective-permute-done.36.kv3
  746.8 7.9 shard_map.135.q_ref
  754.7 12.1 %shard_map.137 = (bf16[1024,512]{1,0:T(8,128)(2,1)}, bf16[2,4096,256]{2,1,0:T(8,128)(2,1)}, bf16[2,4096,256]{2,1,0:T(8,128)(2,1)}) custom-call(s32[9]{0:T(128)} %concatenate.23.bounds_ref, bf16[1024,512]{1,0:T(8,128)(2,1)} %shard_map.135.q_ref, bf16[1024,512]{1,0:T(8,128)(2,1)} %shard_map.136.kv0, ...), custom_call_target="tpu_custom_call", output_to_operand_aliasing={{1}: (7, {}), {2}: (8, {})} | custom-call | flops 4294967296 | bytes 8000000 | tf_op jit(solution)/shard_map/pallas_call | solution.py:139
  766.8 69.1 %shard_map.138 = (bf16[256,2560]{1,0:T(8,128)(2,1)}, bf16[1024,2560]{1,0:T(8,128)(2,1)}) custom-call(bf16[1024,512]{1,0:T(8,128)(2,1)} %get-tuple-element.35.o_ref, bf16[512,1280]{1,0:T(8,128)(2,1)} %copy-done.9, bf16[512,1280]{1,0:T(8,128)(2,1)} %copy-done.13, bf16[512,1280]{1,0:T(8,128)(2,1)} %collective-permute-done.39.a2, bf16[256,1280]{1,0:T(8,128)(2,1)} %copy-done.27, ...), custom_call_target="tpu_custom_call" | custom-call | flops 20000000000 | bytes 20000000 | tf_op jit(solution)/shard_map/pallas_call | solution.py:308
  835.9 157.6 %shard_map.139 = bf16[4096,640]{1,0:T(8,128)(2,1)} custom-call(bf16[1024,2560]{1,0:T(8,128)(2,1)} %get-tuple-element.37.refs_0_, bf16[640,2560]{1,0:T(8,128)(2,1)} %get-tuple-element.53.refs_1_, bf16[640,2560]{1,0:T(8,128)(2,1)} %collective-permute-done.47.refs_2_, bf16[640,2560]{1,0:T(8,128)(2,1)} %collective-permute-done.48.refs_3_, ...), custom_call_target="tpu_custom_call" | custom-call | flops 40265318400 | bytes 50000000 | tf_op jit(solution)/shard_map/pallas_call | solution.py:529
  993.6 5.3 copy.30
  (190 shorter events, 29.5 us)
Async XLA Ops:
  0.7 11.5 %collective-permute-start.3 = (f32[2,4,640]{2,1,0:T(4,128)}, f32[2,4,640]{2,1,0:T(4,128)S(1)}, u32[]{:S(2)}, u32[]{:S(2)}) collective-permute-start(f32[2,4,640]{2,1,0:T(4,128)} %param.21), channel_id=1, source_target_pairs={{0,1},{1,0},{2,3},{3,2},{4,5},{5,4},{6,7},{7,6},{8,9},{9,8},{10,11... | collective-permute-start | bytes 61448 | tf_op jit(solution)/shard_map/ppermute | solution.py:551
  6.0 103.0 %collective-permute-start.7 = (bf16[640,1024]{1,0:T(8,128)(2,1)S(1)}, bf16[640,1024]{1,0:T(8,128)(2,1)}, u32[]{:S(2)}, u32[]{:S(2)}) collective-permute-start(bf16[640,1024]{1,0:T(8,128)(2,1)S(1)} %get-tuple-element.60.w0), channel_id=1, source_target_pairs={{0,2},{1,3},{2,0},{3,1},{4,6},{5,7},{6,4},{7,5},{8,10},{9,11},{10,... | collective-permute-start | bytes 3932168 | tf_op jit(solution)/shard_map/ppermute | solution.py:551
  8.7 56.9 %collective-permute-start.12 = (bf16[512,640]{1,0:T(8,128)(2,1)}, bf16[512,640]{1,0:T(8,128)(2,1)}, u32[]{:S(2)}, u32[]{:S(2)}) collective-permute-start(bf16[512,640]{1,0:T(8,128)(2,1)} %get-tuple-element.62), channel_id=1, source_target_pairs={{0,2},{1,3},{2,0},{3,1},{4,6},{5,7},{6,4},{7,5},{8,10},{9,11},{10,... | collective-permute-start | bytes 1966088 | tf_op jit(solution)/shard_map/ppermute | solution.py:551
  12.2 46.5 %collective-permute-start.1 = (bf16[256,640]{1,0:T(8,128)(2,1)S(1)}, bf16[256,640]{1,0:T(8,128)(2,1)S(1)}, u32[]{:S(2)}, u32[]{:S(2)}) collective-permute-start(bf16[256,640]{1,0:T(8,128)(2,1)S(1)} %get-tuple-element.58), channel_id=1, source_target_pairs={{0,2},{1,3},{2,0},{3,1},{4,6},{5,7},{6,4},{7,5},{8,10},{9,11},{10,... | collective-permute-start | bytes 983048 | tf_op jit(solution)/shard_map/ppermute | solution.py:551
  12.9 52.1 %collective-permute-start.2 = (bf16[256,640]{1,0:T(8,128)(2,1)S(1)}, bf16[256,640]{1,0:T(8,128)(2,1)S(1)}, u32[]{:S(2)}, u32[]{:S(2)}) collective-permute-start(bf16[256,640]{1,0:T(8,128)(2,1)S(1)} %get-tuple-element.55), channel_id=1, source_target_pairs={{0,3},{1,2},{2,1},{3,0},{4,7},{5,6},{6,5},{7,4},{8,11},{9,10},{10,... | collective-permute-start | bytes 983048 | tf_op jit(solution)/shard_map/ppermute | solution.py:551
  14.0 96.7 %collective-permute-start.6 = (bf16[640,1024]{1,0:T(8,128)(2,1)S(1)}, bf16[640,1024]{1,0:T(8,128)(2,1)S(1)}, u32[]{:S(2)}, u32[]{:S(2)}) collective-permute-start(bf16[640,1024]{1,0:T(8,128)(2,1)S(1)} %get-tuple-element.60.w0), channel_id=1, source_target_pairs={{0,1},{1,0},{2,3},{3,2},{4,5},{5,4},{6,7},{7,6},{8,9},{9,8},{10,11... | collective-permute-start | bytes 3932168 | tf_op jit(solution)/shard_map/ppermute | solution.py:551
  58.7 52.1 %collective-permute-start.32 = (bf16[640,1024]{1,0:T(8,128)(2,1)S(1)}, bf16[640,1024]{1,0:T(8,128)(2,1)S(1)}, u32[]{:S(2)}, u32[]{:S(2)}) collective-permute-start(bf16[640,1024]{1,0:T(8,128)(2,1)S(1)} %get-tuple-element.59.w0), channel_id=1, source_target_pairs={{0,2},{1,3},{2,0},{3,1},{4,6},{5,7},{6,4},{7,5},{8,10},{9,11},{10,... | collective-permute-start | bytes 3932168 | tf_op jit(solution)/shard_map/ppermute | solution.py:551
  65.0 46.3 %collective-permute-start.31 = (bf16[640,1024]{1,0:T(8,128)(2,1)S(1)}, bf16[640,1024]{1,0:T(8,128)(2,1)S(1)}, u32[]{:S(2)}, u32[]{:S(2)}) collective-permute-start(bf16[640,1024]{1,0:T(8,128)(2,1)S(1)} %get-tuple-element.59.w0), channel_id=1, source_target_pairs={{0,1},{1,0},{2,3},{3,2},{4,5},{5,4},{6,7},{7,6},{8,9},{9,8},{10,11... | collective-permute-start | bytes 3932168 | tf_op jit(solution)/shard_map/ppermute | solution.py:551
  65.7 41.5 %collective-permute-start.37 = (bf16[512,640]{1,0:T(8,128)(2,1)S(1)}, bf16[512,640]{1,0:T(8,128)(2,1)S(1)}, u32[]{:S(2)}, u32[]{:S(2)}) collective-permute-start(bf16[512,640]{1,0:T(8,128)(2,1)S(1)} %get-tuple-element.61), channel_id=1, source_target_pairs={{0,2},{1,3},{2,0},{3,1},{4,6},{5,7},{6,4},{7,5},{8,10},{9,11},{10,... | collective-permute-start | bytes 1966088 | tf_op jit(solution)/shard_map/ppermute | solution.py:551
  107.2 31.8 %collective-permute-start.13 = (bf16[512,1280]{1,0:T(8,128)(2,1)S(1)}, bf16[512,1280]{1,0:T(8,128)(2,1)}, u32[]{:S(2)}, u32[]{:S(2)}) collective-permute-start(bf16[512,1280]{1,0:T(8,128)(2,1)S(1)} %pad_maximum_fusion.a0), channel_id=1, source_target_pairs={{0,4},{4,0},{8,12},{12,8},{1,5},{5,1},{9,13},{13,9},{2,6},{6,2},{1... | collective-permute-start | bytes 3932168 | tf_op jit(solution)/shard_map/ppermute | solution.py:551
  109.0 31.8 %collective-permute-start.14 = (bf16[512,1280]{1,0:T(8,128)(2,1)S(1)}, bf16[512,1280]{1,0:T(8,128)(2,1)}, u32[]{:S(2)}, u32[]{:S(2)}) collective-permute-start(bf16[512,1280]{1,0:T(8,128)(2,1)S(1)} %pad_maximum_fusion.a0), channel_id=1, source_target_pairs={{0,8},{4,12},{8,0},{12,4},{1,9},{5,13},{9,1},{13,5},{2,10},{6,14},... | collective-permute-start | bytes 3932168 | tf_op jit(solution)/shard_map/ppermute | solution.py:551
  110.7 32.5 %collective-permute-start.17 = (bf16[512,1280]{1,0:T(8,128)(2,1)S(1)}, bf16[512,1280]{1,0:T(8,128)(2,1)S(1)}, u32[]{:S(2)}, u32[]{:S(2)}) collective-permute-start(bf16[512,1280]{1,0:T(8,128)(2,1)S(1)} %pad_maximum_fusion.a0), channel_id=1, source_target_pairs={{0,1},{1,0},{2,3},{3,2},{4,5},{5,4},{6,7},{7,6},{8,9},{9,8},{10,11... | collective-permute-start | bytes 3932168 | tf_op jit(solution)/shard_map/ppermute | solution.py:551
  110.8 54.7 %collective-permute-start.38 = (bf16[512,1280]{1,0:T(8,128)(2,1)S(1)}, bf16[512,1280]{1,0:T(8,128)(2,1)S(1)}, u32[]{:S(2)}, u32[]{:S(2)}) collective-permute-start(bf16[512,1280]{1,0:T(8,128)(2,1)S(1)} %pad_maximum_fusion.1.a0), channel_id=1, source_target_pairs={{0,4},{4,0},{8,12},{12,8},{1,5},{5,1},{9,13},{13,9},{2,6},{6,2},{1... | collective-permute-start | bytes 3932168 | tf_op jit(solution)/shard_map/ppermute | solution.py:551
  111.3 56.0 %collective-permute-start.39 = (bf16[512,1280]{1,0:T(8,128)(2,1)S(1)}, bf16[512,1280]{1,0:T(8,128)(2,1)}, u32[]{:S(2)}, u32[]{:S(2)}) collective-permute-start(bf16[512,1280]{1,0:T(8,128)(2,1)S(1)} %pad_maximum_fusion.1.a0), channel_id=1, source_target_pairs={{0,8},{4,12},{8,0},{12,4},{1,9},{5,13},{9,1},{13,5},{2,10},{6,14},... | collective-permute-start | bytes 3932168 | tf_op jit(solution)/shard_map/ppermute | solution.py:551
  139.0 37.2 %collective-permute-start.42 = (bf16[512,1280]{1,0:T(8,128)(2,1)S(1)}, bf16[512,1280]{1,0:T(8,128)(2,1)S(1)}, u32[]{:S(2)}, u32[]{:S(2)}) collective-permute-start(bf16[512,1280]{1,0:T(8,128)(2,1)S(1)} %pad_maximum_fusion.1.a0), channel_id=1, source_target_pairs={{0,1},{1,0},{2,3},{3,2},{4,5},{5,4},{6,7},{7,6},{8,9},{9,8},{10,11... | collective-permute-start | bytes 3932168 | tf_op jit(solution)/shard_map/ppermute | solution.py:551
  140.8 37.0 %collective-permute-start.8 = (bf16[640,1024]{1,0:T(8,128)(2,1)}, bf16[640,1024]{1,0:T(8,128)(2,1)S(1)}, u32[]{:S(2)}, u32[]{:S(2)}) collective-permute-start(bf16[640,1024]{1,0:T(8,128)(2,1)} %collective-permute-done.7.w2), channel_id=1, source_target_pairs={{0,1},{1,0},{2,3},{3,2},{4,5},{5,4},{6,7},{7,6},{8,9},{9,8},{10,11... | collective-permute-start | bytes 3932168 | tf_op jit(solution)/shard_map/ppermute | solution.py:551
  143.2 44.8 %collective-permute-start.33 = (bf16[640,1024]{1,0:T(8,128)(2,1)S(1)}, bf16[640,1024]{1,0:T(8,128)(2,1)S(1)}, u32[]{:S(2)}, u32[]{:S(2)}) collective-permute-start(bf16[640,1024]{1,0:T(8,128)(2,1)S(1)} %collective-permute-done.32.w2), channel_id=1, source_target_pairs={{0,1},{1,0},{2,3},{3,2},{4,5},{5,4},{6,7},{7,6},{8,9},{9,8},{10,11... | collective-permute-start | bytes 3932168 | tf_op jit(solution)/shard_map/ppermute | solution.py:551
  165.5 17.6 %collective-permute-start.15 = (bf16[256,1280]{1,0:T(8,128)(2,1)S(1)}, bf16[256,1280]{1,0:T(8,128)(2,1)S(1)}, u32[]{:S(2)}, u32[]{:S(2)}) collective-permute-start(bf16[256,1280]{1,0:T(8,128)(2,1)S(1)} %slice.115), channel_id=1, source_target_pairs={{0,8},{4,12},{8,0},{12,4},{1,9},{5,13},{9,1},{13,5},{2,10},{6,14},... | collective-permute-start | bytes 1966088 | tf_op jit(solution)/shard_map/ppermute | solution.py:551
  167.3 17.5 %collective-permute-start.16 = (bf16[256,1280]{1,0:T(8,128)(2,1)S(1)}, bf16[256,1280]{1,0:T(8,128)(2,1)}, u32[]{:S(2)}, u32[]{:S(2)}) collective-permute-start(bf16[256,1280]{1,0:T(8,128)(2,1)S(1)} %slice.116), channel_id=1, source_target_pairs={{0,4},{4,0},{8,12},{12,8},{1,5},{5,1},{9,13},{13,9},{2,6},{6,2},{1... | collective-permute-start | bytes 1966088 | tf_op jit(solution)/shard_map/ppermute | solution.py:551
  176.2 74.1 %collective-permute-start.23 = (bf16[640,2560]{1,0:T(8,128)(2,1)}, bf16[640,2560]{1,0:T(8,128)(2,1)}, u32[]{:S(2)}, u32[]{:S(2)}) collective-permute-start(bf16[640,2560]{1,0:T(8,128)(2,1)} %get-tuple-element.54.g0), channel_id=1, source_target_pairs={{0,2},{1,3},{2,0},{3,1},{4,6},{5,7},{6,4},{7,5},{8,10},{9,11},{10,... | collective-permute-start | bytes 9830408 | tf_op jit(solution)/shard_map/ppermute | solution.py:551
  177.8 17.3 %collective-permute-start.40 = (bf16[256,1280]{1,0:T(8,128)(2,1)S(1)}, bf16[256,1280]{1,0:T(8,128)(2,1)S(1)}, u32[]{:S(2)}, u32[]{:S(2)}) collective-permute-start(bf16[256,1280]{1,0:T(8,128)(2,1)S(1)} %slice.122), channel_id=1, source_target_pairs={{0,8},{4,12},{8,0},{12,4},{1,9},{5,13},{9,1},{13,5},{2,10},{6,14},... | collective-permute-start | bytes 1966088 | tf_op jit(solution)/shard_map/ppermute | solution.py:551
  183.1 13.3 %collective-permute-start.41 = (bf16[256,1280]{1,0:T(8,128)(2,1)S(1)}, bf16[256,1280]{1,0:T(8,128)(2,1)S(1)}, u32[]{:S(2)}, u32[]{:S(2)}) collective-permute-start(bf16[256,1280]{1,0:T(8,128)(2,1)S(1)} %slice.123), channel_id=1, source_target_pairs={{0,4},{4,0},{8,12},{12,8},{1,5},{5,1},{9,13},{13,9},{2,6},{6,2},{1... | collective-permute-start | bytes 1966088 | tf_op jit(solution)/shard_map/ppermute | solution.py:551
  184.9 11.6 %collective-permute-start.20 = (bf16[256,1280]{1,0:T(8,128)(2,1)S(1)}, bf16[256,1280]{1,0:T(8,128)(2,1)S(1)}, u32[]{:S(2)}, u32[]{:S(2)}) collective-permute-start(bf16[256,1280]{1,0:T(8,128)(2,1)S(1)} %collective-permute-done.15.a3), channel_id=1, source_target_pairs={{0,1},{1,0},{2,3},{3,2},{4,5},{5,4},{6,7},{7,6},{8,9},{9,8},{10,11... | collective-permute-start | bytes 1966088 | tf_op jit(solution)/shard_map/ppermute | solution.py:551
  188.1 132.5 %collective-permute-start.26 = (bf16[640,2560]{1,0:T(8,128)(2,1)}, bf16[640,2560]{1,0:T(8,128)(2,1)}, u32[]{:S(2)}, u32[]{:S(2)}) collective-permute-start(bf16[640,2560]{1,0:T(8,128)(2,1)} %get-tuple-element.52.u0), channel_id=1, source_target_pairs={{0,2},{1,3},{2,0},{3,1},{4,6},{5,7},{6,4},{7,5},{8,10},{9,11},{10,... | collective-permute-start | bytes 9830408 | tf_op jit(solution)/shard_map/ppermute | solution.py:551
  202.0 188.8 %collective-permute-start.29 = (bf16[2560,640]{1,0:T(8,128)(2,1)S(1)}, bf16[2560,640]{1,0:T(8,128)(2,1)}, u32[]{:S(2)}, u32[]{:S(2)}) collective-permute-start(bf16[2560,640]{1,0:T(8,128)(2,1)S(1)} %get-tuple-element.50.d0), channel_id=1, source_target_pairs={{0,2},{1,3},{2,0},{3,1},{4,6},{5,7},{6,4},{7,5},{8,10},{9,11},{10,... | collective-permute-start | bytes 9830408 | tf_op jit(solution)/shard_map/ppermute | solution.py:551
  203.6 206.8 %collective-permute-start.22 = (bf16[640,2560]{1,0:T(8,128)(2,1)}, bf16[640,2560]{1,0:T(8,128)(2,1)}, u32[]{:S(2)}, u32[]{:S(2)}) collective-permute-start(bf16[640,2560]{1,0:T(8,128)(2,1)} %get-tuple-element.54.g0), channel_id=1, source_target_pairs={{0,1},{1,0},{2,3},{3,2},{4,5},{5,4},{6,7},{7,6},{8,9},{9,8},{10,11... | collective-permute-start | bytes 9830408 | tf_op jit(solution)/shard_map/ppermute | solution.py:551
  203.7 207.2 %collective-permute-start.25 = (bf16[640,2560]{1,0:T(8,128)(2,1)}, bf16[640,2560]{1,0:T(8,128)(2,1)}, u32[]{:S(2)}, u32[]{:S(2)}) collective-permute-start(bf16[640,2560]{1,0:T(8,128)(2,1)} %get-tuple-element.52.u0), channel_id=1, source_target_pairs={{0,1},{1,0},{2,3},{3,2},{4,5},{5,4},{6,7},{7,6},{8,9},{9,8},{10,11... | collective-permute-start | bytes 9830408 | tf_op jit(solution)/shard_map/ppermute | solution.py:551
  250.4 188.7 %collective-permute-start.28 = (bf16[2560,640]{1,0:T(8,128)(2,1)S(1)}, bf16[2560,640]{1,0:T(8,128)(2,1)}, u32[]{:S(2)}, u32[]{:S(2)}) collective-permute-start(bf16[2560,640]{1,0:T(8,128)(2,1)S(1)} %get-tuple-element.50.d0), channel_id=1, source_target_pairs={{0,1},{1,0},{2,3},{3,2},{4,5},{5,4},{6,7},{7,6},{8,9},{9,8},{10,11... | collective-permute-start | bytes 9830408 | tf_op jit(solution)/shard_map/ppermute | solution.py:551
  320.6 89.8 %collective-permute-start.10 = (bf16[1024,512]{1,0:T(8,128)(2,1)}, bf16[1024,512]{1,0:T(8,128)(2,1)S(1)}, u32[]{:S(2)}, u32[]{:S(2)}) collective-permute-start(bf16[1024,512]{1,0:T(8,128)(2,1)} %shard_map.131.kv0), channel_id=1, source_target_pairs={{0,2},{1,3},{2,0},{3,1},{4,6},{5,7},{6,4},{7,5},{8,10},{9,11},{10,... | collective-permute-start | bytes 3145736 | tf_op jit(solution)/shard_map/ppermute | solution.py:551
  390.8 20.1 %collective-permute-start.9 = (bf16[1024,512]{1,0:T(8,128)(2,1)}, bf16[1024,512]{1,0:T(8,128)(2,1)S(1)}, u32[]{:S(2)}, u32[]{:S(2)}) collective-permute-start(bf16[1024,512]{1,0:T(8,128)(2,1)} %shard_map.131.kv0), channel_id=1, source_target_pairs={{0,1},{1,0},{2,3},{3,2},{4,5},{5,4},{6,7},{7,6},{8,9},{9,8},{10,11... | collective-permute-start | bytes 3145736 | tf_op jit(solution)/shard_map/ppermute | solution.py:551
  410.4 100.0 %collective-permute-start.24 = (bf16[640,2560]{1,0:T(8,128)(2,1)}, bf16[640,2560]{1,0:T(8,128)(2,1)}, u32[]{:S(2)}, u32[]{:S(2)}) collective-permute-start(bf16[640,2560]{1,0:T(8,128)(2,1)} %collective-permute-done.23.g2), channel_id=1, source_target_pairs={{0,1},{1,0},{2,3},{3,2},{4,5},{5,4},{6,7},{7,6},{8,9},{9,8},{10,11... | collective-permute-start | bytes 9830408 | tf_op jit(solution)/shard_map/ppermute | solution.py:551
  410.9 99.7 %collective-permute-start.27 = (bf16[640,2560]{1,0:T(8,128)(2,1)}, bf16[640,2560]{1,0:T(8,128)(2,1)}, u32[]{:S(2)}, u32[]{:S(2)}) collective-permute-start(bf16[640,2560]{1,0:T(8,128)(2,1)} %collective-permute-done.26.u2), channel_id=1, source_target_pairs={{0,1},{1,0},{2,3},{3,2},{4,5},{5,4},{6,7},{7,6},{8,9},{9,8},{10,11... | collective-permute-start | bytes 9830408 | tf_op jit(solution)/shard_map/ppermute | solution.py:551
  411.9 100.6 %collective-permute-start.30 = (bf16[2560,640]{1,0:T(8,128)(2,1)}, bf16[2560,640]{1,0:T(8,128)(2,1)}, u32[]{:S(2)}, u32[]{:S(2)}) collective-permute-start(bf16[2560,640]{1,0:T(8,128)(2,1)} %collective-permute-done.29.d2), channel_id=1, source_target_pairs={{0,1},{1,0},{2,3},{3,2},{4,5},{5,4},{6,7},{7,6},{8,9},{9,8},{10,11... | collective-permute-start | bytes 9830408 | tf_op jit(solution)/shard_map/ppermute | solution.py:551
  415.5 25.8 %collective-permute-start.45 = (bf16[256,1280]{1,0:T(8,128)(2,1)}, bf16[256,1280]{1,0:T(8,128)(2,1)}, u32[]{:S(2)}, u32[]{:S(2)}) collective-permute-start(bf16[256,1280]{1,0:T(8,128)(2,1)} %copy-done.27), channel_id=1, source_target_pairs={{0,1},{1,0},{2,3},{3,2},{4,5},{5,4},{6,7},{7,6},{8,9},{9,8},{10,11... | collective-permute-start | bytes 1966088 | tf_op jit(solution)/shard_map/ppermute | solution.py:551
  439.1 71.4 %collective-permute-start.43 = (bf16[512,1280]{1,0:T(8,128)(2,1)}, bf16[512,1280]{1,0:T(8,128)(2,1)}, u32[]{:S(2)}, u32[]{:S(2)}) collective-permute-start(bf16[512,1280]{1,0:T(8,128)(2,1)} %copy-done.13), channel_id=1, source_target_pairs={{0,1},{1,0},{2,3},{3,2},{4,5},{5,4},{6,7},{7,6},{8,9},{9,8},{10,11... | collective-permute-start | bytes 3932168 | tf_op jit(solution)/shard_map/ppermute | solution.py:551
  441.3 65.8 %collective-permute-start.46 = (bf16[256,1280]{1,0:T(8,128)(2,1)}, bf16[256,1280]{1,0:T(8,128)(2,1)}, u32[]{:S(2)}, u32[]{:S(2)}) collective-permute-start(bf16[256,1280]{1,0:T(8,128)(2,1)} %copy-done.28), channel_id=1, source_target_pairs={{0,1},{1,0},{2,3},{3,2},{4,5},{5,4},{6,7},{7,6},{8,9},{9,8},{10,11... | collective-permute-start | bytes 1966088 | tf_op jit(solution)/shard_map/ppermute | solution.py:551
  507.1 174.4 %collective-permute-start.48 = (bf16[640,2560]{1,0:T(8,128)(2,1)}, bf16[640,2560]{1,0:T(8,128)(2,1)}, u32[]{:S(2)}, u32[]{:S(2)}) collective-permute-start(bf16[640,2560]{1,0:T(8,128)(2,1)} %get-tuple-element.53.refs_1_), channel_id=1, source_target_pairs={{0,2},{1,3},{2,0},{3,1},{4,6},{5,7},{6,4},{7,5},{8,10},{9,11},{10,... | collective-permute-start | bytes 9830408 | tf_op jit(solution)/shard_map/ppermute | solution.py:551
  510.4 233.1 %collective-permute-start.47 = (bf16[640,2560]{1,0:T(8,128)(2,1)}, bf16[640,2560]{1,0:T(8,128)(2,1)}, u32[]{:S(2)}, u32[]{:S(2)}) collective-permute-start(bf16[640,2560]{1,0:T(8,128)(2,1)} %get-tuple-element.53.refs_1_), channel_id=1, source_target_pairs={{0,1},{1,0},{2,3},{3,2},{4,5},{5,4},{6,7},{7,6},{8,9},{9,8},{10,11... | collective-permute-start | bytes 9830408 | tf_op jit(solution)/shard_map/ppermute | solution.py:551
  510.4 232.5 %collective-permute-start.51 = (bf16[640,2560]{1,0:T(8,128)(2,1)}, bf16[640,2560]{1,0:T(8,128)(2,1)}, u32[]{:S(2)}, u32[]{:S(2)}) collective-permute-start(bf16[640,2560]{1,0:T(8,128)(2,1)} %get-tuple-element.51.refs_5_), channel_id=1, source_target_pairs={{0,2},{1,3},{2,0},{3,1},{4,6},{5,7},{6,4},{7,5},{8,10},{9,11},{10,... | collective-permute-start | bytes 9830408 | tf_op jit(solution)/shard_map/ppermute | solution.py:551
  510.5 232.9 %collective-permute-start.54 = (bf16[2560,640]{1,0:T(8,128)(2,1)}, bf16[2560,640]{1,0:T(8,128)(2,1)}, u32[]{:S(2)}, u32[]{:S(2)}) collective-permute-start(bf16[2560,640]{1,0:T(8,128)(2,1)} %get-tuple-element.49.refs_9_), channel_id=1, source_target_pairs={{0,2},{1,3},{2,0},{3,1},{4,6},{5,7},{6,4},{7,5},{8,10},{9,11},{10,... | collective-permute-start | bytes 9830408 | tf_op jit(solution)/shard_map/ppermute | solution.py:551
  512.5 169.0 %collective-permute-start.44 = (bf16[512,1280]{1,0:T(8,128)(2,1)}, bf16[512,1280]{1,0:T(8,128)(2,1)}, u32[]{:S(2)}, u32[]{:S(2)}) collective-permute-start(bf16[512,1280]{1,0:T(8,128)(2,1)} %collective-permute-done.39.a2), channel_id=1, source_target_pairs={{0,1},{1,0},{2,3},{3,2},{4,5},{5,4},{6,7},{7,6},{8,9},{9,8},{10,11... | collective-permute-start | bytes 3932168 | tf_op jit(solution)/shard_map/ppermute | solution.py:551
  681.5 61.4 %collective-permute-start.35 = (bf16[1024,512]{1,0:T(8,128)(2,1)}, bf16[1024,512]{1,0:T(8,128)(2,1)S(1)}, u32[]{:S(2)}, u32[]{:S(2)}) collective-permute-start(bf16[1024,512]{1,0:T(8,128)(2,1)} %shard_map.136.kv0), channel_id=1, source_target_pairs={{0,2},{1,3},{2,0},{3,1},{4,6},{5,7},{6,4},{7,5},{8,10},{9,11},{10,... | collective-permute-start | bytes 3145736 | tf_op jit(solution)/shard_map/ppermute | solution.py:551
  681.5 62.4 %collective-permute-start.34 = (bf16[1024,512]{1,0:T(8,128)(2,1)}, bf16[1024,512]{1,0:T(8,128)(2,1)S(1)}, u32[]{:S(2)}, u32[]{:S(2)}) collective-permute-start(bf16[1024,512]{1,0:T(8,128)(2,1)} %shard_map.136.kv0), channel_id=1, source_target_pairs={{0,1},{1,0},{2,3},{3,2},{4,5},{5,4},{6,7},{7,6},{8,9},{9,8},{10,11... | collective-permute-start | bytes 3145736 | tf_op jit(solution)/shard_map/ppermute | solution.py:551
  742.9 93.0 %collective-permute-start.50 = (bf16[640,2560]{1,0:T(8,128)(2,1)}, bf16[640,2560]{1,0:T(8,128)(2,1)}, u32[]{:S(2)}, u32[]{:S(2)}) collective-permute-start(bf16[640,2560]{1,0:T(8,128)(2,1)} %get-tuple-element.51.refs_5_), channel_id=1, source_target_pairs={{0,1},{1,0},{2,3},{3,2},{4,5},{5,4},{6,7},{7,6},{8,9},{9,8},{10,11... | collective-permute-start | bytes 9830408 | tf_op jit(solution)/shard_map/ppermute | solution.py:551
  743.4 92.5 %collective-permute-start.53 = (bf16[2560,640]{1,0:T(8,128)(2,1)}, bf16[2560,640]{1,0:T(8,128)(2,1)}, u32[]{:S(2)}, u32[]{:S(2)}) collective-permute-start(bf16[2560,640]{1,0:T(8,128)(2,1)} %get-tuple-element.49.refs_9_), channel_id=1, source_target_pairs={{0,1},{1,0},{2,3},{3,2},{4,5},{5,4},{6,7},{7,6},{8,9},{9,8},{10,11... | collective-permute-start | bytes 9830408 | tf_op jit(solution)/shard_map/ppermute | solution.py:551
  743.5 92.4 %collective-permute-start.49 = (bf16[640,2560]{1,0:T(8,128)(2,1)}, bf16[640,2560]{1,0:T(8,128)(2,1)}, u32[]{:S(2)}, u32[]{:S(2)}) collective-permute-start(bf16[640,2560]{1,0:T(8,128)(2,1)} %collective-permute-done.48.refs_3_), channel_id=1, source_target_pairs={{0,1},{1,0},{2,3},{3,2},{4,5},{5,4},{6,7},{7,6},{8,9},{9,8},{10,11... | collective-permute-start | bytes 9830408 | tf_op jit(solution)/shard_map/ppermute | solution.py:551
  743.9 92.0 %collective-permute-start.52 = (bf16[640,2560]{1,0:T(8,128)(2,1)}, bf16[640,2560]{1,0:T(8,128)(2,1)}, u32[]{:S(2)}, u32[]{:S(2)}) collective-permute-start(bf16[640,2560]{1,0:T(8,128)(2,1)} %collective-permute-done.51.refs_7_), channel_id=1, source_target_pairs={{0,1},{1,0},{2,3},{3,2},{4,5},{5,4},{6,7},{7,6},{8,9},{9,8},{10,11... | collective-permute-start | bytes 9830408 | tf_op jit(solution)/shard_map/ppermute | solution.py:551
  745.6 90.4 %collective-permute-start.55 = (bf16[2560,640]{1,0:T(8,128)(2,1)}, bf16[2560,640]{1,0:T(8,128)(2,1)}, u32[]{:S(2)}, u32[]{:S(2)}) collective-permute-start(bf16[2560,640]{1,0:T(8,128)(2,1)} %collective-permute-done.54.refs_11_), channel_id=1, source_target_pairs={{0,1},{1,0},{2,3},{3,2},{4,5},{5,4},{6,7},{7,6},{8,9},{9,8},{10,11... | collective-permute-start | bytes 9830408 | tf_op jit(solution)/shard_map/ppermute | solution.py:551
  (47 other events, 973.4 us)
